TPU v7x, 32 devices: a whole 2x2x4 slice. The times are simulated.
32 devices in a mesh: grp: 8 (over z, x), tbl: 4 (over y, core).
Axes of the slice: x: 2, y: 2, z: 4, core: 2. Of those that a mesh axis runs over, the one named last changes fastest.
Arguments:
- next_ids: int32 [4096, 224], P(('grp', 'tbl')), may hold values from 0 to 6143
- next_lengths: int32 [4096, 26], P(('grp', 'tbl')), may hold values from 1 to 8
- slot_of_table: int32 [26], replicated, may hold values from 0 to 27, as said below
- tables: bfloat16 [28, 6144, 128], P('tbl'), may hold values from -2.5 to 2.5
- cross_input: bfloat16 [4096, 3456], P(('grp', 'tbl')), may hold values from -6 to 6
- cotangent: bfloat16 [4096, 3456], P(('grp', 'tbl')), may hold values from -6 to 6
- up_weight: bfloat16 [256, 3456], replicated, may hold values from -0.375 to 0.375
- down_weight: bfloat16 [3456, 256], replicated, may hold values from -0.109375 to 0.109375
Outputs:
- next_embedded: bfloat16 [4096, 3328], P(('grp', 'tbl'))
- grad_up: float32 [256, 3456], P('tbl', 'grp')
- grad_down: float32 [3456, 256], P('grp', 'tbl')
Inputs may be any that keep to these rules, and one draw needn't show every extreme that they name: `next_ids`: entry 8 * s + k of an example's row is the k-th id of the bag held in slot s; entries with k at or past the bag's length, and all entries of slots that hold no table, are padding. `slot_of_table`: distinct slots; owner o along tbl holds slots o * 7 to o * 7 + 6, so an owner holds up to 7 tables and some owner holds exactly 7.
All inputs are finite; a program needn't handle non-finite values.
Results may differ from a plain program's by a relative error of at most 0.0049.
Values may be sent and summed in bfloat16 or wider, within the bound.
A program may use at most 128 MiB of HBM per device.

v0:
```python
import functools
import math

import jax
import jax.numpy as jnp
from jax import lax
from jax.experimental import pallas as pl
from jax.experimental.pallas import tpu as pltpu
from jax.sharding import PartitionSpec as P

LANES = 128


def pool_kernel(maxlen, idx_ref, tab_ref, out_ref, stage, wide, acc, sem):
    owners, batch, _ = out_ref.shape
    slots, rows, width = tab_ref.shape
    per_line = LANES // maxlen
    lines = batch // per_line
    chunk = 256

    def fetch(s):
        return pltpu.make_async_copy(tab_ref.at[s], stage.at[s % 2], sem.at[s % 2])

    fetch(0).start()
    wide[pl.ds(rows, 8), :] = jnp.zeros((8, width), jnp.float32)
    for s in range(slots):
        if s + 1 < slots:
            fetch(s + 1).start()
        fetch(s).wait()

        @pl.loop(0, rows // chunk)
        def _(c):
            at = pl.ds(pl.multiple_of(c * chunk, chunk), chunk)
            wide[at, :] = stage[s % 2, at, :].astype(jnp.float32)

        @pl.loop(0, owners * lines)
        def _(g):
            src = g // lines
            line = s * lines + g % lines
            for u in range(per_line):
                got = [
                    wide[pl.ds(idx_ref[src, line, u * maxlen + k], 1), :] for k in range(maxlen)
                ]
                while len(got) > 1:
                    got = [a + b for a, b in zip(got[::2], got[1::2])] + (
                        [got[-1]] if len(got) % 2 else []
                    )
                acc[pl.ds(g * per_line + u, 1), :] = got[0]

        for o in range(owners):
            out_ref[o, :, s * width : (s + 1) * width] = acc[
                o * batch : (o + 1) * batch, :
            ].astype(jnp.bfloat16)


def pool(idx, tables, batch, maxlen):
    slots, rows, width = tables.shape
    owners = idx.shape[0]
    return pl.pallas_call(
        functools.partial(pool_kernel, maxlen),
        out_shape=jax.ShapeDtypeStruct((owners, batch, slots * width), jnp.bfloat16),
        in_specs=[
            pl.BlockSpec(memory_space=pltpu.SMEM),
            pl.BlockSpec(memory_space=pl.ANY),
        ],
        out_specs=pl.BlockSpec(memory_space=pltpu.VMEM),
        scratch_shapes=[
            pltpu.VMEM((2, rows, width), jnp.bfloat16),
            pltpu.VMEM((rows + 8, width), jnp.float32),
            pltpu.VMEM((owners * batch, width), jnp.float32),
            pltpu.SemaphoreType.DMA((2,)),
        ],
        compiler_params=pltpu.CompilerParams(vmem_limit_bytes=60 << 20),
        cost_estimate=pl.CostEstimate(
            flops=100_000_000, bytes_accessed=tables.size * 2, transcendentals=0
        ),
        name="pool",
    )(idx, tables)


def order_kernel(slot_ref, got_ref, out_ref):
    owners, batch, wide = got_ref.shape
    feats = slot_ref.shape[0]
    width = out_ref.shape[1] // feats
    slots = wide // width
    for f in range(feats):
        s = slot_ref[f]
        at = pl.ds(pl.multiple_of(lax.rem(s, slots) * width, width), width)
        out_ref[:, f * width : (f + 1) * width] = got_ref[lax.div(s, slots), :, at]


def order(slot_of_table, got, width):
    return pl.pallas_call(
        order_kernel,
        out_shape=jax.ShapeDtypeStruct(
            (got.shape[1], slot_of_table.shape[0] * width), jnp.bfloat16
        ),
        in_specs=[
            pl.BlockSpec(memory_space=pltpu.SMEM),
            pl.BlockSpec(memory_space=pltpu.VMEM),
        ],
        out_specs=pl.BlockSpec(memory_space=pltpu.VMEM),
        name="order",
    )(slot_of_table, got)


def bag_rows(next_ids, next_lengths, slot_of_table, slots, owners, rows):
    batch = next_ids.shape[0]
    slots_all = slots * owners
    maxlen = next_ids.shape[1] // slots_all
    hit = (slot_of_table[:, None] == lax.broadcasted_iota(jnp.int32, (1, slots_all), 1)).astype(
        jnp.int32
    )
    slot_lengths = jnp.sum(next_lengths[:, :, None] * hit[None, :, :], axis=1)
    keep = lax.broadcasted_iota(jnp.int32, (batch, slots_all, maxlen), 2) < slot_lengths[:, :, None]
    idx = jnp.where(keep, next_ids.reshape(batch, slots_all, maxlen), rows)
    return idx.transpose(1, 0, 2).reshape(owners, slots * batch * maxlen // LANES, LANES)


def plain(
    next_ids, next_lengths, slot_of_table, tables, cross_input, cotangent, up_weight, down_weight
):
    batch = next_ids.shape[0]
    owners = lax.axis_size("tbl")
    slots, rows, width = tables.shape
    maxlen = next_ids.shape[1] // (slots * owners)
    idx = bag_rows(next_ids, next_lengths, slot_of_table, slots, owners, rows)
    low = jnp.dot(cross_input, down_weight, preferred_element_type=jnp.float32).astype(jnp.bfloat16)
    dz = (cotangent.astype(jnp.float32) * cross_input.astype(jnp.float32)).astype(jnp.bfloat16)
    dlow = jnp.dot(dz, up_weight.T, preferred_element_type=jnp.float32).astype(jnp.bfloat16)
    total = batch * lax.axis_size("grp") * owners
    factor = 1.0 / math.sqrt(total)
    part_up = jnp.dot(low.T, dz, preferred_element_type=jnp.float32) * factor
    part_down = jnp.dot(cross_input.T, dlow, preferred_element_type=jnp.float32) * factor
    part_up, part_down = part_up.astype(jnp.bfloat16), part_down.astype(jnp.bfloat16)
    owner_up, owner_down = (
        lax.psum_scatter(part_up, "tbl", scatter_dimension=0, tiled=True).astype(jnp.float32),
        lax.psum_scatter(part_down, "tbl", scatter_dimension=1, tiled=True).astype(jnp.float32),
    )
    got_idx = lax.all_to_all(idx, "tbl", split_axis=0, concat_axis=0, tiled=True)
    pooled = pool(got_idx, tables, batch, maxlen)
    returned = lax.all_to_all(pooled, "tbl", split_axis=0, concat_axis=0, tiled=True)
    next_embedded = order(slot_of_table, returned, width)
    grad_up, grad_down = (
        lax.psum_scatter(owner_up, "grp", scatter_dimension=1, tiled=True),
        lax.psum_scatter(owner_down, "grp", scatter_dimension=0, tiled=True),
    )
    return (next_embedded, grad_up, grad_down)


def step_kernel(
    maxlen,
    factor,
    split,
    checkpoints,
    ids_ref,
    len_ref,
    slot_ref,
    tab_ref,
    x_hbm,
    ct_hbm,
    up_hbm,
    down_hbm,
    emb_ref,
    grad_up_ref,
    grad_down_ref,
    x_ref,
    ct_ref,
    up_ref,
    down_ref,
    idx_ref,
    idx_in,
    turned,
    idx_s,
    part,
    c_in,
    a_in,
    b_in,
    a2_in,
    b2_in,
    z_in,
    stage,
    wide,
    acc,
    pooled,
    got,
    tab_sem,
    smem_sem,
    idx_sem,
    core_sem,
    one_sem,
    two_sem,
    z_sem,
    pool_sem,
    load_sem,
):
    owners, zs, _, high, lanes = part.shape
    slots, rows, width = tab_ref.shape
    batch = x_ref.shape[0]
    rank = down_ref.shape[1]
    cols = rank // owners
    group = 32
    chunk = 1024 if rows % 1024 == 0 else 256
    g, t = lax.axis_index("grp"), lax.axis_index("tbl")
    z, x = g // 2, g % 2
    core = t + 1 - 2 * (t % 2)
    far = (t + 2) % owners
    other = 1 - x
    side = g + 1 - 2 * x

    def fetch(s):
        return pltpu.make_async_copy(tab_ref.at[s], stage.at[s % 2], tab_sem.at[s % 2])

    def send(src, dst, sems, n, device):
        return pltpu.make_async_remote_copy(
            src_ref=src,
            dst_ref=dst,
            send_sem=sems.at[0, n],
            recv_sem=sems.at[1, n],
            device_id=device,
            device_id_type=pl.DeviceIdType.MESH,
        )

    loads = [
        pltpu.make_async_copy(a, b, load_sem.at[n])
        for n, (a, b) in enumerate(
            ((x_hbm, x_ref), (down_hbm, down_ref), (ct_hbm, ct_ref), (up_hbm, up_ref))
        )
    ]
    for copy in loads:
        copy.start()
    fetch(0).start()
    barrier = pltpu.get_barrier_semaphore()
    near = [(g, (t + d) % owners) for d in range(1, owners)] + [(side, t)]
    near += [((z + d) % zs * 2 + x, t) for d in range(1, zs)]
    for device in near:
        pl.semaphore_signal(
            barrier, inc=1, device_id=device, device_id_type=pl.DeviceIdType.MESH
        )

    feats, span = slot_ref.shape[0], ids_ref.shape[0]
    each = slots * maxlen
    feat = lax.broadcasted_iota(jnp.int32, (span, feats), 1)
    entry = lax.broadcasted_iota(jnp.int32, (span, feats), 0)
    held_by = jnp.zeros((span, feats), jnp.int32)
    for f in range(feats):
        held_by = jnp.where(feat == f, slot_ref[f], held_by)
    hit = jnp.where(held_by == entry // maxlen, 1.0, 0.0).astype(jnp.bfloat16)
    lens = jnp.dot(
        hit, len_ref[...].astype(jnp.float32).astype(jnp.bfloat16), preferred_element_type=jnp.float32
    )
    place = (lax.broadcasted_iota(jnp.int32, (span, batch), 0) % maxlen).astype(jnp.float32)
    idx = jnp.where(place < lens, ids_ref[...], rows)
    for o in range(owners):
        idx_ref[o] = idx[o * each : (o + 1) * each]

    pl.semaphore_wait(barrier, len(near))

    ids_out = [
        send(idx_ref.at[(t + d) % owners], idx_in.at[t], idx_sem, d - 1, (g, (t + d) % owners))
        for d in range(1, owners)
    ]
    for copy in ids_out:
        copy.start()

    loads[0].wait()
    loads[1].wait()
    low = jnp.dot(x_ref[...], down_ref[...], preferred_element_type=jnp.float32).astype(jnp.bfloat16)
    loads[2].wait()
    dz = (ct_ref[...].astype(jnp.float32) * x_ref[...].astype(jnp.float32)).astype(jnp.bfloat16)
    loads[3].wait()
    dlow = lax.dot_general(
        dz, up_ref[...], (((1,), (1,)), ((), ())), preferred_element_type=jnp.float32
    ).astype(jnp.bfloat16)
    first = (((0,), (0,)), ((), ()))
    for block in range(2 * zs):
        begin = block * high
        edge = begin // LANES * LANES
        stop = -(-(begin + high) // LANES) * LANES
        up = lax.dot_general(dz[:, edge:stop], low, first, preferred_element_type=jnp.float32)
        down = lax.dot_general(
            x_ref[:, edge:stop], dlow, first, preferred_element_type=jnp.float32
        )
        up = (up[begin - edge : begin - edge + high] * factor).astype(jnp.bfloat16)
        down = (down[begin - edge : begin - edge + high] * factor).astype(jnp.bfloat16)
        for o in range(owners):
            part[o, block // 2, block % 2] = jnp.concatenate(
                [up[:, o * cols : (o + 1) * cols], down[:, o * cols : (o + 1) * cols]], axis=1
            )

    cross = [
        send(part.at[core], c_in.at[0], core_sem, 0, (g, core)),
        send(part.at[(core + 2) % owners], c_in.at[1], core_sem, 1, (g, core)),
    ]
    for copy in cross:
        copy.start()

    for copy in ids_out:
        copy.wait()
    idx_in[t] = idx_ref[t]
    for o in range(owners):
        turned[o] = jnp.zeros((batch, LANES), jnp.int32)
        turned[o, :, :each] = idx_in[o].T
    got_ids = [
        pltpu.make_async_copy(
            turned.at[o], idx_s.at[pl.ds(o * batch, batch)], smem_sem.at[o]
        )
        for o in range(owners)
    ]
    for copy in got_ids:
        copy.start()
    for copy in got_ids:
        copy.wait()

    low_rows, high_rows = pl.ds(0, split), pl.ds(split, high - split)

    def add(where, value):
        part[where] = (part[where].astype(jnp.float32) + value.astype(jnp.float32)).astype(
            jnp.bfloat16
        )

    one = [
        send(part.at[far, :, :, low_rows], a_in, one_sem, 0, (g, far)),
        send(part.at[t, :, other, high_rows], b_in.at[0], one_sem, 1, (side, t)),
        send(part.at[far, :, other, high_rows], b_in.at[1], one_sem, 2, (side, t)),
    ]
    two = [
        send(part.at[t, :, other, low_rows], a2_in, two_sem, 0, (side, t)),
        send(part.at[far, :, x, high_rows], b2_in, two_sem, 1, (g, far)),
    ]
    last = [
        send(
            part.at[t, (z + d) % zs, x], z_in.at[d - 1], z_sem, d - 1, ((z + d) % zs * 2 + x, t)
        )
        for d in range(1, zs)
    ]

    def after_core():
        for copy in cross:
            copy.wait()
        for n, o in ((1, far), (0, t)):
            for k in range(zs):
                for j in range(2):
                    add((o, k, j), c_in[n, k, j])
        for copy in one:
            copy.start()

    def after_one():
        for copy in one:
            copy.wait()
        for k in range(zs):
            add((t, k, other, low_rows), a_in[k, other])
            add((far, k, x, high_rows), b_in[1, k])
        for copy in two:
            copy.start()
        for k in range(zs):
            add((t, k, x, low_rows), a_in[k, x])
            add((t, k, x, high_rows), b_in[0, k])

    def after_two():
        for copy in two:
            copy.wait()
        for k in range(zs):
            add((t, k, x, low_rows), a2_in[k])
            add((t, k, x, high_rows), b2_in[k])
        for copy in last:
            copy.start()

    stages = [after_core, after_one, after_two]
    returns = []
    wide[pl.ds(rows, 8), :] = jnp.zeros((8, width), jnp.float32)
    for s in range(slots):
        if s + 1 < slots:
            fetch(s + 1).start()
        fetch(s).wait()

        @pl.loop(0, rows // chunk)
        def _(c):
            at = pl.ds(pl.multiple_of(c * chunk, chunk), chunk)
            wide[at, :] = stage[s % 2, at, :].astype(jnp.float32)

        @pl.loop(0, owners * batch // group)
        def _(i):
            for u in range(group):
                held = [
                    wide[pl.ds(idx_s[i * group + u, s * maxlen + k], 1), :] for k in range(maxlen)
                ]
                while len(held) > 1:
                    held = [a + b for a, b in zip(held[::2], held[1::2])] + (
                        [held[-1]] if len(held) % 2 else []
                    )
                acc[pl.ds(i * group + u, 1), :] = held[0]

        for n, at in enumerate(checkpoints):
            if at == s:
                stages[n]()
        got[t, s] = acc[pl.ds(pl.multiple_of(t * batch, batch), batch), :].astype(jnp.bfloat16)
        for d in range(1, owners):
            o = (t + d) % owners
            pooled[d - 1, s] = acc[pl.ds(pl.multiple_of(o * batch, batch), batch), :].astype(
                jnp.bfloat16
            )
            copy = send(
                pooled.at[d - 1, s], got.at[t, s], pool_sem, s * (owners - 1) + d - 1, (g, o)
            )
            copy.start()
            returns.append(copy)

    for copy in last:
        copy.wait()
    total = part[t, z, x].astype(jnp.float32)
    for d in range(1, zs):
        total += z_in[d - 1].astype(jnp.float32)
    total = total.T
    grad_up_ref[...] = total[:cols]
    grad_down_ref[...] = total[cols:]
    for copy in returns:
        copy.wait()
    for f in range(slot_ref.shape[0]):
        s = slot_ref[f]
        emb_ref[:, f * width : (f + 1) * width] = got[lax.div(s, slots), lax.rem(s, slots)]


def fused_step(
    next_ids, next_lengths, slot_of_table, tables, cross_input, cotangent, up_weight, down_weight, maxlen, factor
):
    groups, owners = lax.axis_size("grp"), lax.axis_size("tbl")
    slots, rows, width = tables.shape
    batch, depth = cross_input.shape
    zs, high = groups // 2, depth // groups
    split = (high // 2 + 15) // 16 * 16
    sems = pltpu.SemaphoreType.DMA
    bf16 = jnp.bfloat16
    any_space = pl.BlockSpec(memory_space=pl.ANY)
    idx_shape = (owners, next_ids.shape[1] // owners, batch)
    half = down_weight.shape[1] // owners
    vmem = pl.BlockSpec(memory_space=pltpu.VMEM)
    checkpoints = (0, min(3, slots - 1), min(5, slots - 1))
    return pl.pallas_call(
        functools.partial(step_kernel, maxlen, factor, split, checkpoints),
        out_shape=(
            jax.ShapeDtypeStruct((batch, slot_of_table.shape[0] * width), bf16),
            jax.ShapeDtypeStruct((half, high), jnp.float32),
            jax.ShapeDtypeStruct((half, high), jnp.float32),
        ),
        in_specs=[
            vmem,
            vmem,
            pl.BlockSpec(memory_space=pltpu.SMEM),
            any_space,
            any_space,
            any_space,
            any_space,
            any_space,
        ],
        out_specs=(vmem, vmem, vmem),
        scratch_shapes=[
            pltpu.VMEM(cross_input.shape, bf16),
            pltpu.VMEM(cotangent.shape, bf16),
            pltpu.VMEM(up_weight.shape, bf16),
            pltpu.VMEM(down_weight.shape, bf16),
            pltpu.VMEM(idx_shape, jnp.int32),
            pltpu.VMEM(idx_shape, jnp.int32),
            pltpu.VMEM((owners, batch, LANES), jnp.int32),
            pltpu.SMEM((owners * batch, LANES), jnp.int32),
            pltpu.VMEM((owners, zs, 2, high, LANES), bf16),
            pltpu.VMEM((2, zs, 2, high, LANES), bf16),
            pltpu.VMEM((zs, 2, split, LANES), bf16),
            pltpu.VMEM((2, zs, high - split, LANES), bf16),
            pltpu.VMEM((zs, split, LANES), bf16),
            pltpu.VMEM((zs, high - split, LANES), bf16),
            pltpu.VMEM((max(zs - 1, 1), high, LANES), bf16),
            pltpu.VMEM((2, rows, width), bf16),
            pltpu.VMEM((rows + 8, width), jnp.float32),
            pltpu.VMEM((owners * batch, width), jnp.float32),
            pltpu.VMEM((owners - 1, slots, batch, width), bf16),
            pltpu.VMEM((owners, slots, batch, width), bf16),
            sems((2,)),
            sems((owners,)),
            sems((2, owners - 1)),
            sems((2, 2)),
            sems((2, 3)),
            sems((2, 2)),
            sems((2, max(zs - 1, 1))),
            sems((2, slots * (owners - 1))),
            sems((4,)),
        ],
        compiler_params=pltpu.CompilerParams(
            collective_id=0, has_side_effects=True, vmem_limit_bytes=56 << 20
        ),
        name="fused_step",
    )(
        next_ids.T,
        next_lengths.T,
        slot_of_table,
        tables,
        cross_input,
        cotangent,
        up_weight,
        down_weight,
    )


def on_device(
    next_ids, next_lengths, slot_of_table, tables, cross_input, cotangent, up_weight, down_weight
):
    groups, owners = lax.axis_size("grp"), lax.axis_size("tbl")
    batch, depth = cross_input.shape
    rank = down_weight.shape[1]
    slots, rows, _ = tables.shape
    maxlen = next_ids.shape[1] // (slots * owners)
    fits = owners == 4 and groups % 2 == 0 and depth % (16 * groups) == 0 and batch % 16 == 0
    if not fits or rank * 2 != owners * LANES or slots * maxlen % 8 or slots * maxlen > LANES or batch != LANES:
        return plain(
            next_ids,
            next_lengths,
            slot_of_table,
            tables,
            cross_input,
            cotangent,
            up_weight,
            down_weight,
        )
    factor = 1.0 / math.sqrt(batch * groups * owners)
    next_embedded, grad_up, grad_down = fused_step(
        next_ids,
        next_lengths,
        slot_of_table,
        tables,
        cross_input,
        cotangent,
        up_weight,
        down_weight,
        maxlen,
        factor,
    )
    return next_embedded, grad_up, grad_down.T


def solution(mesh):
    return jax.shard_map(
        on_device,
        mesh=mesh,
        in_specs=(
            P(("grp", "tbl"), None),
            P(("grp", "tbl"), None),
            P(),
            P("tbl", None, None),
            P(("grp", "tbl"), None),
            P(("grp", "tbl"), None),
            P(),
            P(),
        ),
        out_specs=(P(("grp", "tbl"), None), P("tbl", "grp"), P("grp", "tbl")),
        check_vma=False,
    )
```

profile of v0, /device:TPU:0, one launch (start us, length us, event | category | flops | bytes accessed | tf_op | source)
XLA Modules:
  0.0 55.1 jit_solution(12863984214265374937)
XLA Ops:
  0.6 50.9 %fused_step.1 = (bf16[128,3328]{1,0:T(8,128)(2,1)}, f32[64,432]{1,0:T(8,128)}, f32[64,432]{1,0:T(8,128)}) custom-call(s32[224,128]{1,0:T(8,128)} %bitcast.4, s32[26,128]{1,0:T(8,128)} %bitcast.5, s32[26]{0:T(128)} %slot_ref.1, bf16[7,6144,128]{2,1,0:T(8,128)(2,1)} %tab_ref.1, bf16[128,3456]{1,0:T(8,128)(2,1)} %x_hbm.1, bf16[128,3456]{1,0:T(8,128)(2,1)} %ct_hbm.1, ...), custom_call_target="tpu_custom_call" | custom-call | tf_op jit(solution)/shard_map/fused_step/pallas_call | solution.py:439
  51.6 0.0 copy-start.1
  51.6 0.0 copy-start
  51.6 2.2 %copy.14 = bf16[128,3328]{1,0:T(8,128)(2,1)} copy(bf16[128,3328]{1,0:T(8,128)(2,1)} %get-tuple-element.12) | data formatting | bytes 1703936
  53.8 0.0 copy-done.1
  53.8 0.7 %copy.15 = f32[64,432]{1,0:T(8,128)} copy(f32[64,432]{1,0:T(8,128)S(1)} %copy-done.1) | data formatting | bytes 221184
  54.4 0.0 copy-done
  54.4 0.7 %copy.16 = f32[432,64]{0,1:T(8,128)} copy(f32[432,64]{0,1:T(8,128)S(1)} %bitcast.3) | data formatting | bytes 221184
Async XLA Ops:
  51.6 2.2 %copy-start.1 = (f32[64,432]{1,0:T(8,128)S(1)}, f32[64,432]{1,0:T(8,128)}, u32[]{:S(2)}) copy-start(f32[64,432]{1,0:T(8,128)} %get-tuple-element.13) | copy-start | bytes 331780
  51.6 2.8 %copy-start = (f32[64,432]{1,0:T(8,128)S(1)}, f32[64,432]{1,0:T(8,128)}, u32[]{:S(2)}) copy-start(f32[64,432]{1,0:T(8,128)} %get-tuple-element.8) | copy-start | bytes 331780
where the time goes:
time: 55.2 us; the launch traced here: 55.1 us
  Pallas kernels  50.9 us (92%)
  local copies, waits for them, and re-layouts  3.47 us (6%)
  between operations  0.66 us (1%)
    pallas_call x1, Pallas kernels, fused_step(): pl.pallas_call(functools.partial(step_kernel, maxlen, factor, split, chec...  50.9 us
    unnamed x7, local copies, waits for them, and re-layouts  3.47 us

commit v1 on v0

--- a/solution.py
+++ b/solution.py
@@ -170,7 +170,6 @@
     down_ref,
     idx_ref,
     idx_in,
-    turned,
     idx_s,
     part,
     c_in,
@@ -180,7 +179,8 @@
     b2_in,
     z_in,
     stage,
-    wide,
+    wide_even,
+    wide_odd,
     acc,
     pooled,
     got,
@@ -199,7 +199,6 @@
     batch = x_ref.shape[0]
     rank = down_ref.shape[1]
     cols = rank // owners
-    group = 32
     chunk = 1024 if rows % 1024 == 0 else 256
     g, t = lax.axis_index("grp"), lax.axis_index("tbl")
     z, x = g // 2, g % 2
@@ -254,15 +253,6 @@
     for o in range(owners):
         idx_ref[o] = idx[o * each : (o + 1) * each]
 
-    pl.semaphore_wait(barrier, len(near))
-
-    ids_out = [
-        send(idx_ref.at[(t + d) % owners], idx_in.at[t], idx_sem, d - 1, (g, (t + d) % owners))
-        for d in range(1, owners)
-    ]
-    for copy in ids_out:
-        copy.start()
-
     loads[0].wait()
     loads[1].wait()
     low = jnp.dot(x_ref[...], down_ref[...], preferred_element_type=jnp.float32).astype(jnp.bfloat16)
@@ -272,6 +262,15 @@
     dlow = lax.dot_general(
         dz, up_ref[...], (((1,), (1,)), ((), ())), preferred_element_type=jnp.float32
     ).astype(jnp.bfloat16)
+    pl.semaphore_wait(barrier, len(near))
+
+    ids_out = [
+        send(idx_ref.at[(t + d) % owners], idx_in.at[t], idx_sem, d - 1, (g, (t + d) % owners))
+        for d in range(1, owners)
+    ]
+    for copy in ids_out:
+        copy.start()
+
     first = (((0,), (0,)), ((), ()))
     for block in range(2 * zs):
         begin = block * high
@@ -298,19 +297,24 @@
     for copy in ids_out:
         copy.wait()
     idx_in[t] = idx_ref[t]
-    for o in range(owners):
-        turned[o] = jnp.zeros((batch, LANES), jnp.int32)
-        turned[o, :, :each] = idx_in[o].T
+
+    def peer(j):
+        return (t // 2 + 1 - j // 2) % 2 * 2 + (t + (j + 1) // 2) % 2
+
     got_ids = [
-        pltpu.make_async_copy(
-            turned.at[o], idx_s.at[pl.ds(o * batch, batch)], smem_sem.at[o]
-        )
-        for o in range(owners)
-    ]
-    for copy in got_ids:
-        copy.start()
-    for copy in got_ids:
-        copy.wait()
+        [
+            pltpu.make_async_copy(
+                idx_in.at[peer(j), pl.ds(s * maxlen, maxlen)],
+                idx_s.at[s, j],
+                smem_sem.at[s * owners + j],
+            )
+            for j in range(owners)
+        ]
+        for s in range(slots)
+    ]
+    for copies in got_ids:
+        for copy in copies:
+            copy.start()
 
     low_rows, high_rows = pl.ds(0, split), pl.ds(split, high - split)
 
@@ -367,44 +371,55 @@
             copy.start()
 
     stages = [after_core, after_one, after_two]
-    returns = []
-    wide[pl.ds(rows, 8), :] = jnp.zeros((8, width), jnp.float32)
+    wides = (wide_even, wide_odd)
+
+    def widen(s, at):
+        wides[s % 2][at, :] = stage[s % 2, at, :].astype(jnp.float32)
+
+    def give(s, j):
+        return send(pooled.at[j, s], got.at[t, s], pool_sem, s * (owners - 1) + j, (g, peer(j)))
+
+    for wide in wides:
+        wide[pl.ds(rows, 8), :] = jnp.zeros((8, width), jnp.float32)
+    fetch(1).start()
+    fetch(0).wait()
+
+    @pl.loop(0, rows // chunk)
+    def _(c):
+        widen(0, pl.ds(pl.multiple_of(c * chunk, chunk), chunk))
+
+    share = rows // owners
     for s in range(slots):
+        for copy in got_ids[s]:
+            copy.wait()
         if s + 1 < slots:
-            fetch(s + 1).start()
-        fetch(s).wait()
-
-        @pl.loop(0, rows // chunk)
-        def _(c):
-            at = pl.ds(pl.multiple_of(c * chunk, chunk), chunk)
-            wide[at, :] = stage[s % 2, at, :].astype(jnp.float32)
-
-        @pl.loop(0, owners * batch // group)
-        def _(i):
-            for u in range(group):
-                held = [
-                    wide[pl.ds(idx_s[i * group + u, s * maxlen + k], 1), :] for k in range(maxlen)
-                ]
+            fetch(s + 1).wait()
+        if s + 2 < slots:
+            fetch(s + 2).start()
+        wide = wides[s % 2]
+
+        @pl.loop(0, owners)
+        def _(j):
+            if s + 1 < slots:
+                widen(s + 1, pl.ds(pl.multiple_of(j * share, share), share))
+            ids = [idx_s.at[s, j, k] for k in range(maxlen)]
+            for u in range(batch):
+                held = [wide[pl.ds(ids[k][u], 1), :] for k in range(maxlen)]
                 while len(held) > 1:
                     held = [a + b for a, b in zip(held[::2], held[1::2])] + (
                         [held[-1]] if len(held) % 2 else []
                     )
-                acc[pl.ds(i * group + u, 1), :] = held[0]
+                acc[pl.ds(u, 1), :] = held[0]
+            pooled[j, s] = acc[...].astype(jnp.bfloat16)
+
+            @pl.when(j < owners - 1)
+            def _():
+                give(s, j).start()
 
         for n, at in enumerate(checkpoints):
             if at == s:
                 stages[n]()
-        got[t, s] = acc[pl.ds(pl.multiple_of(t * batch, batch), batch), :].astype(jnp.bfloat16)
-        for d in range(1, owners):
-            o = (t + d) % owners
-            pooled[d - 1, s] = acc[pl.ds(pl.multiple_of(o * batch, batch), batch), :].astype(
-                jnp.bfloat16
-            )
-            copy = send(
-                pooled.at[d - 1, s], got.at[t, s], pool_sem, s * (owners - 1) + d - 1, (g, o)
-            )
-            copy.start()
-            returns.append(copy)
+        got[t, s] = pooled[owners - 1, s]
 
     for copy in last:
         copy.wait()
@@ -414,8 +429,9 @@
     total = total.T
     grad_up_ref[...] = total[:cols]
     grad_down_ref[...] = total[cols:]
-    for copy in returns:
-        copy.wait()
+    for s in range(slots):
+        for j in range(owners - 1):
+            give(s, j).wait()
     for f in range(slot_ref.shape[0]):
         s = slot_ref[f]
         emb_ref[:, f * width : (f + 1) * width] = got[lax.div(s, slots), lax.rem(s, slots)]
@@ -461,8 +477,7 @@
             pltpu.VMEM(down_weight.shape, bf16),
             pltpu.VMEM(idx_shape, jnp.int32),
             pltpu.VMEM(idx_shape, jnp.int32),
-            pltpu.VMEM((owners, batch, LANES), jnp.int32),
-            pltpu.SMEM((owners * batch, LANES), jnp.int32),
+            pltpu.SMEM((slots, owners, maxlen, batch), jnp.int32),
             pltpu.VMEM((owners, zs, 2, high, LANES), bf16),
             pltpu.VMEM((2, zs, 2, high, LANES), bf16),
             pltpu.VMEM((zs, 2, split, LANES), bf16),
@@ -472,11 +487,12 @@
             pltpu.VMEM((max(zs - 1, 1), high, LANES), bf16),
             pltpu.VMEM((2, rows, width), bf16),
             pltpu.VMEM((rows + 8, width), jnp.float32),
-            pltpu.VMEM((owners * batch, width), jnp.float32),
-            pltpu.VMEM((owners - 1, slots, batch, width), bf16),
+            pltpu.VMEM((rows + 8, width), jnp.float32),
+            pltpu.VMEM((batch, width), jnp.float32),
+            pltpu.VMEM((owners, slots, batch, width), bf16),
             pltpu.VMEM((owners, slots, batch, width), bf16),
             sems((2,)),
-            sems((owners,)),
+            sems((slots * owners,)),
             sems((2, owners - 1)),
             sems((2, 2)),
             sems((2, 3)),
@@ -510,7 +526,7 @@
     slots, rows, _ = tables.shape
     maxlen = next_ids.shape[1] // (slots * owners)
     fits = owners == 4 and groups % 2 == 0 and depth % (16 * groups) == 0 and batch % 16 == 0
-    if not fits or rank * 2 != owners * LANES or slots * maxlen % 8 or slots * maxlen > LANES or batch != LANES:
+    if not fits or rank * 2 != owners * LANES or slots * maxlen % 8 or maxlen != 8 or rows % 1024 or batch != LANES:
         return plain(
             next_ids,
             next_lengths,

time: 55.2 us -> 52.4 us (0.949)
  Pallas kernels: 50.9 us -> 48.1 us
    pallas_call x1, Pallas kernels: 50.9 us -> 48.1 us  [fused_step(): pl.pallas_call(functools.partial(step_kernel, maxlen, factor, split, chec...]
where the time goes in v1:
time: 52.4 us; the launch traced here: 52.2 us
  Pallas kernels  48.1 us (92%)
  local copies, waits for them, and re-layouts  3.47 us (7%)
  between operations  0.66 us (1%)
    pallas_call x1, Pallas kernels, fused_step(): pl.pallas_call(functools.partial(step_kernel, maxlen, factor, split, chec...  48.1 us
    unnamed x7, local copies, waits for them, and re-layouts  3.47 us

profile of v1, /device:TPU:0, one launch (start us, length us, event | category | flops | bytes accessed | tf_op | source)
XLA Modules:
  0.0 52.2 jit_solution(2639566081601519012)
XLA Ops:
  0.6 48.1 %fused_step.1 = (bf16[128,3328]{1,0:T(8,128)(2,1)}, f32[64,432]{1,0:T(8,128)}, f32[64,432]{1,0:T(8,128)}) custom-call(s32[224,128]{1,0:T(8,128)} %bitcast.4, s32[26,128]{1,0:T(8,128)} %bitcast.5, s32[26]{0:T(128)} %slot_ref.1, bf16[7,6144,128]{2,1,0:T(8,128)(2,1)} %tab_ref.1, bf16[128,3456]{1,0:T(8,128)(2,1)} %x_hbm.1, bf16[128,3456]{1,0:T(8,128)(2,1)} %ct_hbm.1, ...), custom_call_target="tpu_custom_call" | custom-call | tf_op jit(solution)/shard_map/fused_step/pallas_call | solution.py:455
  48.7 0.0 copy-start.1
  48.7 0.0 copy-start
  48.7 2.2 %copy.14 = bf16[128,3328]{1,0:T(8,128)(2,1)} copy(bf16[128,3328]{1,0:T(8,128)(2,1)} %get-tuple-element.12) | data formatting | bytes 1703936
  50.9 0.0 copy-done.1
  50.9 0.7 %copy.15 = f32[64,432]{1,0:T(8,128)} copy(f32[64,432]{1,0:T(8,128)S(1)} %copy-done.1) | data formatting | bytes 221184
  51.5 0.0 copy-done
  51.5 0.7 %copy.16 = f32[432,64]{0,1:T(8,128)} copy(f32[432,64]{0,1:T(8,128)S(1)} %bitcast.3) | data formatting | bytes 221184
Async XLA Ops:
  48.7 2.2 %copy-start.1 = (f32[64,432]{1,0:T(8,128)S(1)}, f32[64,432]{1,0:T(8,128)}, u32[]{:S(2)}) copy-start(f32[64,432]{1,0:T(8,128)} %get-tuple-element.13) | copy-start | bytes 331780
  48.7 2.8 %copy-start = (f32[64,432]{1,0:T(8,128)S(1)}, f32[64,432]{1,0:T(8,128)}, u32[]{:S(2)}) copy-start(f32[64,432]{1,0:T(8,128)} %get-tuple-element.8) | copy-start | bytes 331780

commit v2 on v1

v2 whole, which is shorter than its diff:
```python
import functools
import itertools
import math

import jax
import jax.numpy as jnp
from jax import lax
from jax.experimental import pallas as pl
from jax.experimental.pallas import tpu as pltpu
from jax.sharding import PartitionSpec as P

LANES = 128


def pool_kernel(maxlen, idx_ref, tab_ref, out_ref, stage, wide, acc, sem):
    owners, batch, _ = out_ref.shape
    slots, rows, width = tab_ref.shape
    per_line = LANES // maxlen
    lines = batch // per_line
    chunk = 256

    def fetch(s):
        return pltpu.make_async_copy(tab_ref.at[s], stage.at[s % 2], sem.at[s % 2])

    fetch(0).start()
    wide[pl.ds(rows, 8), :] = jnp.zeros((8, width), jnp.float32)
    for s in range(slots):
        if s + 1 < slots:
            fetch(s + 1).start()
        fetch(s).wait()

        @pl.loop(0, rows // chunk)
        def _(c):
            at = pl.ds(pl.multiple_of(c * chunk, chunk), chunk)
            wide[at, :] = stage[s % 2, at, :].astype(jnp.float32)

        @pl.loop(0, owners * lines)
        def _(g):
            src = g // lines
            line = s * lines + g % lines
            for u in range(per_line):
                got = [
                    wide[pl.ds(idx_ref[src, line, u * maxlen + k], 1), :] for k in range(maxlen)
                ]
                while len(got) > 1:
                    got = [a + b for a, b in zip(got[::2], got[1::2])] + (
                        [got[-1]] if len(got) % 2 else []
                    )
                acc[pl.ds(g * per_line + u, 1), :] = got[0]

        for o in range(owners):
            out_ref[o, :, s * width : (s + 1) * width] = acc[
                o * batch : (o + 1) * batch, :
            ].astype(jnp.bfloat16)


def pool(idx, tables, batch, maxlen):
    slots, rows, width = tables.shape
    owners = idx.shape[0]
    return pl.pallas_call(
        functools.partial(pool_kernel, maxlen),
        out_shape=jax.ShapeDtypeStruct((owners, batch, slots * width), jnp.bfloat16),
        in_specs=[
            pl.BlockSpec(memory_space=pltpu.SMEM),
            pl.BlockSpec(memory_space=pl.ANY),
        ],
        out_specs=pl.BlockSpec(memory_space=pltpu.VMEM),
        scratch_shapes=[
            pltpu.VMEM((2, rows, width), jnp.bfloat16),
            pltpu.VMEM((rows + 8, width), jnp.float32),
            pltpu.VMEM((owners * batch, width), jnp.float32),
            pltpu.SemaphoreType.DMA((2,)),
        ],
        compiler_params=pltpu.CompilerParams(vmem_limit_bytes=60 << 20),
        cost_estimate=pl.CostEstimate(
            flops=100_000_000, bytes_accessed=tables.size * 2, transcendentals=0
        ),
        name="pool",
    )(idx, tables)


def order_kernel(slot_ref, got_ref, out_ref):
    owners, batch, wide = got_ref.shape
    feats = slot_ref.shape[0]
    width = out_ref.shape[1] // feats
    slots = wide // width
    for f in range(feats):
        s = slot_ref[f]
        at = pl.ds(pl.multiple_of(lax.rem(s, slots) * width, width), width)
        out_ref[:, f * width : (f + 1) * width] = got_ref[lax.div(s, slots), :, at]


def order(slot_of_table, got, width):
    return pl.pallas_call(
        order_kernel,
        out_shape=jax.ShapeDtypeStruct(
            (got.shape[1], slot_of_table.shape[0] * width), jnp.bfloat16
        ),
        in_specs=[
            pl.BlockSpec(memory_space=pltpu.SMEM),
            pl.BlockSpec(memory_space=pltpu.VMEM),
        ],
        out_specs=pl.BlockSpec(memory_space=pltpu.VMEM),
        name="order",
    )(slot_of_table, got)


def bag_rows(next_ids, next_lengths, slot_of_table, slots, owners, rows):
    batch = next_ids.shape[0]
    slots_all = slots * owners
    maxlen = next_ids.shape[1] // slots_all
    hit = (slot_of_table[:, None] == lax.broadcasted_iota(jnp.int32, (1, slots_all), 1)).astype(
        jnp.int32
    )
    slot_lengths = jnp.sum(next_lengths[:, :, None] * hit[None, :, :], axis=1)
    keep = lax.broadcasted_iota(jnp.int32, (batch, slots_all, maxlen), 2) < slot_lengths[:, :, None]
    idx = jnp.where(keep, next_ids.reshape(batch, slots_all, maxlen), rows)
    return idx.transpose(1, 0, 2).reshape(owners, slots * batch * maxlen // LANES, LANES)


def plain(
    next_ids, next_lengths, slot_of_table, tables, cross_input, cotangent, up_weight, down_weight
):
    batch = next_ids.shape[0]
    owners = lax.axis_size("tbl")
    slots, rows, width = tables.shape
    maxlen = next_ids.shape[1] // (slots * owners)
    idx = bag_rows(next_ids, next_lengths, slot_of_table, slots, owners, rows)
    low = jnp.dot(cross_input, down_weight, preferred_element_type=jnp.float32).astype(jnp.bfloat16)
    dz = (cotangent.astype(jnp.float32) * cross_input.astype(jnp.float32)).astype(jnp.bfloat16)
    dlow = jnp.dot(dz, up_weight.T, preferred_element_type=jnp.float32).astype(jnp.bfloat16)
    total = batch * lax.axis_size("grp") * owners
    factor = 1.0 / math.sqrt(total)
    part_up = jnp.dot(low.T, dz, preferred_element_type=jnp.float32) * factor
    part_down = jnp.dot(cross_input.T, dlow, preferred_element_type=jnp.float32) * factor
    part_up, part_down = part_up.astype(jnp.bfloat16), part_down.astype(jnp.bfloat16)
    owner_up, owner_down = (
        lax.psum_scatter(part_up, "tbl", scatter_dimension=0, tiled=True).astype(jnp.float32),
        lax.psum_scatter(part_down, "tbl", scatter_dimension=1, tiled=True).astype(jnp.float32),
    )
    got_idx = lax.all_to_all(idx, "tbl", split_axis=0, concat_axis=0, tiled=True)
    pooled = pool(got_idx, tables, batch, maxlen)
    returned = lax.all_to_all(pooled, "tbl", split_axis=0, concat_axis=0, tiled=True)
    next_embedded = order(slot_of_table, returned, width)
    grad_up, grad_down = (
        lax.psum_scatter(owner_up, "grp", scatter_dimension=1, tiled=True),
        lax.psum_scatter(owner_down, "grp", scatter_dimension=0, tiled=True),
    )
    return (next_embedded, grad_up, grad_down)


PLAN = (("uxyv", 5), ("yuxv", 3), ("xyuv", 2), ("xuvy", 4))
POLLS = ((12, 3, 0), (13, 0, 0), (15, 2, 0), (15, 1, 0), (21, 3, 1), (22, 2, 1), (23, 1, 1), (23, 0, 1), (28, 1, 2), (28, 2, 2), (28, 0, 2), (28, 3, 2), (28, 2, 3), (28, 3, 3), (28, 1, 3), (28, 0, 3))
LATE = ((2, 7),)


def step_kernel(
    maxlen,
    ids_hbm,
    len_hbm,
    slot_hbm,
    tab_ref,
    x_hbm,
    ct_hbm,
    up_hbm,
    down_hbm,
    got,
    out_ref,
    ids_ref,
    len_ref,
    slot_ref,
    x_ref,
    ct_ref,
    up_ref,
    down_ref,
    xt,
    dzt,
    x_in,
    dz_in,
    low_ref,
    dlow_ref,
    low_in,
    dlow_in,
    idx_ref,
    idx_in,
    idx_s,
    part,
    fin,
    fin_out,
    fin_in,
    full,
    stage,
    wide_even,
    wide_odd,
    acc,
    pooled,
    tab_sem,
    smem_sem,
    idx_sem,
    mate_sem,
    class_sem,
    fin_sem,
    pool_sem,
    load_sem,
    *landing,
):
    slots, rows, width = tab_ref.shape
    batch, depth = x_ref.shape
    rank = down_ref.shape[1]
    half = x_in.shape[1]
    owners, groups = 4, 8
    high = depth // groups
    cols = rank // owners
    chunk = 1024
    g, t = lax.axis_index("grp"), lax.axis_index("tbl")
    core = t % 2
    at_axis = {"y": t // 2, "v": g // 4, "u": g // 2 % 2, "x": g % 2}
    mate = (g, t + 1 - 2 * core)
    across = {
        "y": (g, (t + 2) % owners),
        "v": ((g + 4) % groups, t),
        "u": (g + 2 - 4 * at_axis["u"], t),
        "x": (g + 1 - 2 * at_axis["x"], t),
    }

    def fetch(s):
        return pltpu.make_async_copy(tab_ref.at[s], stage.at[s % 2], tab_sem.at[s % 2])

    def send(src, dst, sems, n, device):
        return pltpu.make_async_remote_copy(
            src_ref=src,
            dst_ref=dst,
            send_sem=sems.at[0, n],
            recv_sem=sems.at[1, n],
            device_id=device,
            device_id_type=pl.DeviceIdType.MESH,
        )

    loads = [
        pltpu.make_async_copy(a, b, load_sem.at[n])
        for n, (a, b) in enumerate(
            (
                (ids_hbm, ids_ref),
                (len_hbm, len_ref),
                (slot_hbm, slot_ref),
                (x_hbm, x_ref),
                (down_hbm, down_ref),
                (ct_hbm, ct_ref),
                (up_hbm, up_ref),
            )
        )
    ]
    for copy in loads:
        copy.start()
    fetch(0).start()
    barrier = pltpu.get_barrier_semaphore()
    near = [(g, (t + d) % owners) for d in range(1, owners)] + [across[d] for d in "vux"]
    for device in near:
        pl.semaphore_signal(
            barrier, inc=1, device_id=device, device_id_type=pl.DeviceIdType.MESH
        )

    for copy in loads[:3]:
        copy.wait()
    feats, span = slot_ref.shape[1], ids_ref.shape[0]
    each = slots * maxlen
    entry = lax.broadcasted_iota(jnp.int32, (span, feats), 0)
    hit = jnp.where(slot_ref[...] == entry // maxlen, 1.0, 0.0).astype(jnp.bfloat16)
    lens = jnp.dot(
        hit, len_ref[...].astype(jnp.float32).astype(jnp.bfloat16), preferred_element_type=jnp.float32
    )
    place = (lax.broadcasted_iota(jnp.int32, (span, batch), 0) % maxlen).astype(jnp.float32)
    idx = jnp.where(place < lens, ids_ref[...], rows)
    for o in range(owners):
        idx_ref[o] = idx[o * each : (o + 1) * each]

    def turn(src, dst):
        for n in range(depth // LANES):
            at = slice(n * LANES, (n + 1) * LANES)
            dst[at, :] = src[:, at].T

    loads[3].wait()
    turn(x_ref, xt)
    loads[4].wait()
    low_ref[...] = jnp.dot(
        x_ref[...], down_ref[...], preferred_element_type=jnp.float32
    ).astype(jnp.bfloat16)

    pl.semaphore_wait(barrier, len(near))

    ids_out = [
        send(idx_ref.at[(t + d) % owners], idx_in.at[t], idx_sem, d - 1, (g, (t + d) % owners))
        for d in range(1, owners)
    ]

    def lend(src, dst, n):
        return [
            send(
                src.at[pl.ds(pl.multiple_of(b * high + (1 - core) * (high - half), 16), half)],
                dst.at[b],
                mate_sem,
                n + b,
                mate,
            )
            for b in range(groups)
        ]

    x_out, dz_out = lend(xt, x_in, 0), lend(dzt, dz_in, groups)
    low_out = send(low_ref, low_in, mate_sem, 2 * groups, mate)
    dlow_out = send(dlow_ref, dlow_in, mate_sem, 2 * groups + 1, mate)
    for copy in ids_out + x_out + [low_out]:
        copy.start()

    loads[5].wait()
    ct_ref[...] = (ct_ref[...].astype(jnp.float32) * x_ref[...].astype(jnp.float32)).astype(
        jnp.bfloat16
    )
    turn(ct_ref, dzt)
    for copy in dz_out:
        copy.start()
    loads[6].wait()
    dlow = lax.dot_general(
        ct_ref[...], up_ref[...], (((1,), (1,)), ((), ())), preferred_element_type=jnp.float32
    ).astype(jnp.bfloat16)
    swap = [n + 1 - 2 * (n % 2) for n in range(owners)]
    dlow_ref[...] = jnp.concatenate([dlow[:, n * cols : (n + 1) * cols] for n in swap], axis=1)
    dlow_out.start()

    wides = (wide_even, wide_odd)

    def widen(s, at):
        wides[s % 2][at, :] = stage[s % 2, at, :].astype(jnp.float32)

    for wide in wides:
        wide[pl.ds(rows, 8), :] = jnp.zeros((8, width), jnp.float32)
    fetch(1).start()
    fetch(0).wait()

    @pl.loop(0, rows // chunk)
    def _(c):
        widen(0, pl.ds(pl.multiple_of(c * chunk, chunk), chunk))

    for copy in ids_out:
        copy.wait()
    idx_in[t] = idx_ref[t]

    def peer(j):
        return (t // 2 + 1 - j // 2) % 2 * 2 + (t + (j + 1) // 2) % 2

    got_ids = [
        [
            pltpu.make_async_copy(
                idx_in.at[peer(j), pl.ds(s * maxlen, maxlen)],
                idx_s.at[s, j],
                smem_sem.at[s * owners + j],
            )
            for j in range(owners)
        ]
        for s in range(slots)
    ]
    for copies in got_ids:
        for copy in copies:
            copy.start()

    for copy in x_out + dz_out + [low_out, dlow_out]:
        copy.wait()
    low_two = jnp.concatenate([low_ref[...], low_in[...]], axis=0)
    dlow_two = jnp.concatenate([dlow_ref[...], dlow_in[...]], axis=0)
    left = lax.broadcasted_iota(jnp.int32, (half, LANES), 1) < cols
    for b in range(groups):
        at = pl.ds(pl.multiple_of(b * high + core * (high - half), 16), half)
        up = jnp.dot(
            jnp.concatenate([dzt[at, :], dz_in[b]], axis=1),
            low_two,
            preferred_element_type=jnp.float32,
        )
        down = jnp.dot(
            jnp.concatenate([xt[at, :], x_in[b]], axis=1),
            dlow_two,
            preferred_element_type=jnp.float32,
        )
        for y in range(2):
            u, d = up[:, y * LANES : (y + 1) * LANES], down[:, y * LANES : (y + 1) * LANES]
            part[y, 0, b // 4, b // 2 % 2, b % 2] = jnp.where(left, u, d).astype(jnp.bfloat16)
            part[y, 1, b // 4, b // 2 % 2, b % 2] = jnp.where(left, d, u).astype(jnp.bfloat16)

    begins = [sum(n for _, n in PLAN[:k]) * half // 14 for k in range(len(PLAN) + 1)]

    def place_of(k, held):
        span = pl.ds(begins[k], begins[k + 1] - begins[k])
        return tuple(held.get(d, slice(None)) for d in "ycvux") + (span,)

    def exchange(k, i):
        order = PLAN[k][0]
        held = {d: at_axis[d] for d in order[:i]}
        held[order[i]] = 1 - at_axis[order[i]]
        return send(
            part.at[place_of(k, held)], landing[4 * k + i], class_sem, 4 * k + i, across[order[i]]
        )

    def hand(k):
        span = pl.ds(begins[k], begins[k + 1] - begins[k])
        return send(fin_out.at[span], fin_in.at[span], fin_sem, k, mate)

    def take(k, i):
        exchange(k, i).wait()
        order, came = PLAN[k][0], landing[4 * k + i]
        held = {d: at_axis[d] for d in order[: i + 1]}
        span = pl.ds(begins[k], begins[k + 1] - begins[k])
        if i == 3:
            for c, keep in ((1 - core, False), (core, True)):
                total = part[place_of(k, held | {"c": c})].astype(jnp.float32) + came[c].astype(
                    jnp.float32
                )
                if keep:
                    fin[span, :] = total
                else:
                    fin_out[span, :] = total.astype(jnp.bfloat16)
                    hand(k).start()
            return
        free = [d for d in "ycvux" if d not in held]
        for pick in itertools.product(range(2), repeat=len(free)):
            at = place_of(k, held | dict(zip(free, pick)))
            part[at] = (part[at].astype(jnp.float32) + came[pick].astype(jnp.float32)).astype(
                jnp.bfloat16
            )
        exchange(k, i + 1).start()

    for k in range(len(PLAN)):
        if k not in dict(LATE):
            exchange(k, 0).start()

    def give(s, j):
        return send(pooled.at[j, s], got.at[t, s], pool_sem, s * (owners - 1) + j, (g, peer(j)))

    share = rows // owners
    for s in range(slots):
        for copy in got_ids[s]:
            copy.wait()
        if s + 1 < slots:
            fetch(s + 1).wait()
        if s + 2 < slots:
            fetch(s + 2).start()
        wide = wides[s % 2]

        @pl.loop(0, owners)
        def _(j):
            if s + 1 < slots:
                widen(s + 1, pl.ds(pl.multiple_of(j * share, share), share))
            ids = [idx_s.at[s, j, k] for k in range(maxlen)]
            for u in range(batch):
                held = [wide[pl.ds(ids[k][u], 1), :] for k in range(maxlen)]
                while len(held) > 1:
                    held = [a + b for a, b in zip(held[::2], held[1::2])]
                acc[pl.ds(u, 1), :] = held[0]
            pooled[j, s] = acc[...].astype(jnp.bfloat16)

            @pl.when(j < owners - 1)
            def _():
                give(s, j).start()

            for n in range(owners):
                now = s * owners + n
                todo = [p for p in POLLS if p[0] == now]
                begin = [k for k, p in LATE if p == now]
                if todo or begin:

                    @pl.when(j == n)
                    def _():
                        for _, k, i in todo:
                            take(k, i)
                        for k in begin:
                            exchange(k, 0).start()

        got[t, s] = pooled[owners - 1, s]

    for now, k, i in POLLS:
        if now >= slots * owners:
            take(k, i)
    for k in range(len(PLAN)):
        hand(k).wait()
    other = pl.ds(pl.multiple_of((1 - core) * (high - half), 16), half)
    own = pl.ds(pl.multiple_of(core * (high - half), 16), half)
    full[other, :] = fin_in[...].astype(jnp.float32)
    full[own, :] = fin[...]
    total = full[...].T
    out_ref[core] = total[:cols]
    out_ref[1 - core] = total[cols:]
    for s in range(slots):
        for j in range(owners - 1):
            give(s, j).wait()


def fused_step(
    next_ids, next_lengths, slot_of_table, tables, cross_input, cotangent, up_weight, down_weight, maxlen
):
    groups, owners = lax.axis_size("grp"), lax.axis_size("tbl")
    slots, rows, width = tables.shape
    batch, depth = cross_input.shape
    rank = down_weight.shape[1]
    high = depth // groups
    half = (high // 2 + 15) // 16 * 16
    sems = pltpu.SemaphoreType.DMA
    bf16, f32 = jnp.bfloat16, jnp.float32
    any_space = pl.BlockSpec(memory_space=pl.ANY)
    idx_shape = (owners, next_ids.shape[1] // owners, batch)
    vmem = pl.BlockSpec(memory_space=pltpu.VMEM)
    landing = [
        pltpu.VMEM((2,) * (4 - i) + (n * half // 14, LANES), bf16)
        for _, n in PLAN
        for i in range(4)
    ]
    return pl.pallas_call(
        functools.partial(step_kernel, maxlen),
        out_shape=(
            jax.ShapeDtypeStruct((owners, slots, batch, width), bf16),
            jax.ShapeDtypeStruct((2, rank // owners, high), f32),
        ),
        in_specs=[any_space] * 8,
        out_specs=(vmem, vmem),
        scratch_shapes=[
            pltpu.VMEM(next_ids.shape[::-1], jnp.int32),
            pltpu.VMEM(next_lengths.shape[::-1], jnp.int32),
            pltpu.VMEM((1, slot_of_table.shape[0]), jnp.int32),
            pltpu.VMEM(cross_input.shape, bf16),
            pltpu.VMEM(cotangent.shape, bf16),
            pltpu.VMEM(up_weight.shape, bf16),
            pltpu.VMEM(down_weight.shape, bf16),
            pltpu.VMEM((depth, batch), bf16),
            pltpu.VMEM((depth, batch), bf16),
            pltpu.VMEM((groups, half, batch), bf16),
            pltpu.VMEM((groups, half, batch), bf16),
            pltpu.VMEM((batch, rank), bf16),
            pltpu.VMEM((batch, rank), bf16),
            pltpu.VMEM((batch, rank), bf16),
            pltpu.VMEM((batch, rank), bf16),
            pltpu.VMEM(idx_shape, jnp.int32),
            pltpu.VMEM(idx_shape, jnp.int32),
            pltpu.SMEM((slots, owners, maxlen, batch), jnp.int32),
            pltpu.VMEM((2, 2, 2, 2, 2, half, LANES), bf16),
            pltpu.VMEM((half, LANES), f32),
            pltpu.VMEM((half, LANES), bf16),
            pltpu.VMEM((half, LANES), bf16),
            pltpu.VMEM((high, LANES), f32),
            pltpu.VMEM((2, rows, width), bf16),
            pltpu.VMEM((rows + 8, width), f32),
            pltpu.VMEM((rows + 8, width), f32),
            pltpu.VMEM((batch, width), f32),
            pltpu.VMEM((owners, slots, batch, width), bf16),
            sems((2,)),
            sems((slots * owners,)),
            sems((2, owners - 1)),
            sems((2, 2 * groups + 2)),
            sems((2, 4 * len(PLAN))),
            sems((2, len(PLAN))),
            sems((2, slots * (owners - 1))),
            sems((7,)),
        ]
        + landing,
        compiler_params=pltpu.CompilerParams(
            collective_id=0, has_side_effects=True, vmem_limit_bytes=48 << 20
        ),
        name="fused_step",
    )(
        next_ids.T,
        next_lengths.T,
        slot_of_table[None, :],
        tables,
        cross_input,
        cotangent,
        up_weight,
        down_weight,
    )


def finish_kernel(factor, slot_ref, got_ref, sum_ref, emb_ref, grad_up_ref, grad_down_ref):
    slots, _, width = got_ref.shape[1:]
    for f in range(slot_ref.shape[0]):
        s = slot_ref[f]
        emb_ref[:, f * width : (f + 1) * width] = got_ref[lax.div(s, slots), lax.rem(s, slots)]
    grad_up_ref[...] = sum_ref[0] * factor
    grad_down_ref[...] = sum_ref[1] * factor


def finish(slot_of_table, got, sums, factor):
    _, _, batch, width = got.shape
    vmem = pl.BlockSpec(memory_space=pltpu.VMEM)
    return pl.pallas_call(
        functools.partial(finish_kernel, factor),
        out_shape=(
            jax.ShapeDtypeStruct((batch, slot_of_table.shape[0] * width), jnp.bfloat16),
            jax.ShapeDtypeStruct(sums.shape[1:], jnp.float32),
            jax.ShapeDtypeStruct(sums.shape[1:], jnp.float32),
        ),
        in_specs=[pl.BlockSpec(memory_space=pltpu.SMEM), vmem, vmem],
        out_specs=(vmem, vmem, vmem),
        name="finish",
    )(slot_of_table, got, sums)


def on_device(
    next_ids, next_lengths, slot_of_table, tables, cross_input, cotangent, up_weight, down_weight
):
    groups, owners = lax.axis_size("grp"), lax.axis_size("tbl")
    batch, depth = cross_input.shape
    rank = down_weight.shape[1]
    slots, rows, _ = tables.shape
    maxlen = next_ids.shape[1] // (slots * owners)
    fits = (
        owners == 4
        and groups == 8
        and depth % (16 * groups) == 0
        and depth % LANES == 0
        and depth // groups <= 448
        and depth // groups > 432 - 16
        and rank == 256
        and maxlen == 8
        and slots > 2
        and rows % 1024 == 0
        and batch == LANES
    )
    args = (
        next_ids,
        next_lengths,
        slot_of_table,
        tables,
        cross_input,
        cotangent,
        up_weight,
        down_weight,
    )
    if not fits:
        return plain(*args)
    got, sums = fused_step(*args, maxlen)
    factor = 1.0 / math.sqrt(batch * groups * owners)
    next_embedded, grad_up, grad_down = finish(slot_of_table, got, sums, factor)
    return next_embedded, grad_up, grad_down.T


def solution(mesh):
    return jax.shard_map(
        on_device,
        mesh=mesh,
        in_specs=(
            P(("grp", "tbl"), None),
            P(("grp", "tbl"), None),
            P(),
            P("tbl", None, None),
            P(("grp", "tbl"), None),
            P(("grp", "tbl"), None),
            P(),
            P(),
        ),
        out_specs=(P(("grp", "tbl"), None), P("tbl", "grp"), P("grp", "tbl")),
        check_vma=False,
    )
```

time: 52.4 us -> 48.6 us (0.927)
  Pallas kernels: 48.1 us -> 39.8 us
  local copies, waits for them, and re-layouts: 3.47 us -> 7.72 us
    pallas_call x1 -> x2, Pallas kernels: 48.1 us -> 39.8 us  [the longest x1 37.4 us: fused_step(): pl.pallas_call(functools.partial(step_kernel, maxlen), out_shape=(jax.Sha...]
    unnamed x7 -> x16, local copies, waits for them, and re-layouts: 3.47 us -> 7.72 us
where the time goes in v2:
time: 48.6 us; the launch traced here: 48.2 us
  Pallas kernels  39.8 us (82%)
  local copies, waits for them, and re-layouts  7.72 us (16%)
  between operations  0.66 us (1%)
    pallas_call x1, Pallas kernels, fused_step(): pl.pallas_call(functools.partial(step_kernel, maxlen), out_shape=(jax.Sha...  37.4 us
    unnamed x16, local copies, waits for them, and re-layouts  7.72 us
    pallas_call x1, Pallas kernels, finish(): pl.pallas_call(functools.partial(finish_kernel, factor), out_shape=(jax.S...  2.45 us

profile of v2, /device:TPU:0, one launch (start us, length us, event | category | flops | bytes accessed | tf_op | source)
XLA Modules:
  0.0 48.2 jit_solution(6173463975331417948)
XLA Ops:
  0.6 0.0 copy-start
  0.6 1.5 %copy-done = bf16[256,3456]{1,0:T(8,128)(2,1)S(1)} copy-done((bf16[256,3456]{1,0:T(8,128)(2,1)S(1)}, bf16[256,3456]{1,0:T(8,128)(2,1)}, u32[]{:S(2)}) %copy-start) | copy-done | bytes 1769496
  2.1 0.0 copy-start.2
  2.1 1.2 %copy-done.2 = bf16[128,3456]{1,0:T(8,128)(2,1)S(1)} copy-done((bf16[128,3456]{1,0:T(8,128)(2,1)S(1)}, bf16[128,3456]{1,0:T(8,128)(2,1)}, u32[]{:S(2)}) %copy-start.2) | copy-done | bytes 884760
  3.3 0.0 copy-start.3
  3.3 1.2 %copy-done.3 = bf16[128,3456]{1,0:T(8,128)(2,1)S(1)} copy-done((bf16[128,3456]{1,0:T(8,128)(2,1)S(1)}, bf16[128,3456]{1,0:T(8,128)(2,1)}, u32[]{:S(2)}) %copy-start.3) | copy-done | bytes 884760
  4.4 0.0 copy-start.5
  4.4 0.9 %copy-done.5 = s32[128,224]{0,1:T(8,128)S(1)} copy-done((s32[128,224]{0,1:T(8,128)S(1)}, s32[128,224]{0,1:T(8,128)}, u32[]{:S(2)}) %copy-start.5) | copy-done | bytes 114712
  5.3 0.0 copy-start.6
  5.3 0.7 %copy-done.6 = s32[128,26]{0,1:T(8,128)S(1)} copy-done((s32[128,26]{0,1:T(8,128)S(1)}, s32[128,26]{0,1:T(8,128)}, u32[]{:S(2)}) %copy-start.6) | copy-done | bytes 13336
  6.1 0.0 copy-start.7
  6.1 0.7 %copy-done.7 = s32[26]{0:T(128)S(1)} copy-done((s32[26]{0:T(128)S(1)}, s32[26]{0:T(128)}, u32[]{:S(2)}) %copy-start.7) | copy-done | bytes 128
  6.7 37.4 %fused_step.1 = (bf16[4,7,128,128]{3,2,1,0:T(8,128)(2,1)S(1)}, f32[2,64,432]{2,1,0:T(8,128)S(1)}) custom-call(s32[224,128]{1,0:T(8,128)S(1)} %bitcast.4, s32[26,128]{1,0:T(8,128)S(1)} %bitcast.5, s32[1,26]{1,0:T(1,128)S(1)} %bitcast.6, bf16[7,6144,128]{2,1,0:T(8,128)(2,1)} %tab_ref.1, bf16[128,3456]{1,0:T(8,128)(2,1)S(1)} %copy-done.2, ...), custom_call_target="tpu_custom_call" | custom-call | tf_op jit(solution)/shard_map/fused_step/pallas_call | solution.py:513
  44.1 0.0 copy-start.1
  44.1 0.9 %copy-done.1 = bf16[4,7,128,128]{3,2,1,0:T(8,128)(2,1)} copy-done((bf16[4,7,128,128]{3,2,1,0:T(8,128)(2,1)}, bf16[4,7,128,128]{3,2,1,0:T(8,128)(2,1)S(1)}, u32[]{:S(2)}) %copy-start.1) | copy-done | bytes 917528
  45.0 0.0 copy-start.4
  45.0 0.7 %copy-done.4 = f32[2,64,432]{2,1,0:T(8,128)} copy-done((f32[2,64,432]{2,1,0:T(8,128)}, f32[2,64,432]{2,1,0:T(8,128)S(1)}, u32[]{:S(2)}) %copy-start.4) | copy-done | bytes 221208
  45.8 2.5 %finish.1 = (bf16[128,3328]{1,0:T(8,128)(2,1)}, f32[64,432]{1,0:T(8,128)}, f32[64,432]{1,0:T(8,128)}) custom-call(s32[26]{0:T(128)} %slot_ref.1, bf16[4,7,128,128]{3,2,1,0:T(8,128)(2,1)} %copy-done.1, f32[2,64,432]{2,1,0:T(8,128)} %copy-done.4), custom_call_target="tpu_custom_call" | custom-call | tf_op jit(solution)/shard_map/finish/pallas_call | solution.py:588
Async XLA Ops:
  0.6 1.5 %copy-start = (bf16[256,3456]{1,0:T(8,128)(2,1)S(1)}, bf16[256,3456]{1,0:T(8,128)(2,1)}, u32[]{:S(2)}) copy-start(bf16[256,3456]{1,0:T(8,128)(2,1)} %up_hbm.1) | copy-start | bytes 5308420
  2.1 1.2 %copy-start.2 = (bf16[128,3456]{1,0:T(8,128)(2,1)S(1)}, bf16[128,3456]{1,0:T(8,128)(2,1)}, u32[]{:S(2)}) copy-start(bf16[128,3456]{1,0:T(8,128)(2,1)} %x_hbm.1) | copy-start | bytes 2654212
  3.3 1.2 %copy-start.3 = (bf16[128,3456]{1,0:T(8,128)(2,1)S(1)}, bf16[128,3456]{1,0:T(8,128)(2,1)}, u32[]{:S(2)}) copy-start(bf16[128,3456]{1,0:T(8,128)(2,1)} %ct_hbm.1) | copy-start | bytes 2654212
  4.4 0.9 %copy-start.5 = (s32[128,224]{0,1:T(8,128)S(1)}, s32[128,224]{0,1:T(8,128)}, u32[]{:S(2)}) copy-start(s32[128,224]{0,1:T(8,128)} %param.8) | copy-start | bytes 344068
  5.3 0.7 %copy-start.6 = (s32[128,26]{0,1:T(8,128)S(1)}, s32[128,26]{0,1:T(8,128)}, u32[]{:S(2)}) copy-start(s32[128,26]{0,1:T(8,128)} %param.9) | copy-start | bytes 39940
  6.1 0.7 %copy-start.7 = (s32[26]{0:T(128)S(1)}, s32[26]{0:T(128)}, u32[]{:S(2)}) copy-start(s32[26]{0:T(128)} %slot_ref.1) | copy-start | bytes 316
  44.1 0.9 %copy-start.1 = (bf16[4,7,128,128]{3,2,1,0:T(8,128)(2,1)}, bf16[4,7,128,128]{3,2,1,0:T(8,128)(2,1)S(1)}, u32[]{:S(2)}) copy-start(bf16[4,7,128,128]{3,2,1,0:T(8,128)(2,1)S(1)} %get-tuple-element.8.got_ref) | copy-start | bytes 2752516
  45.0 0.7 %copy-start.4 = (f32[2,64,432]{2,1,0:T(8,128)}, f32[2,64,432]{2,1,0:T(8,128)S(1)}, u32[]{:S(2)}) copy-start(f32[2,64,432]{2,1,0:T(8,128)S(1)} %get-tuple-element.9.sum_ref) | copy-start | bytes 663556

commit v3 on v2

--- a/solution.py
+++ b/solution.py
@@ -156,6 +156,7 @@
 
 def step_kernel(
     maxlen,
+    factor,
     ids_hbm,
     len_hbm,
     slot_hbm,
@@ -484,15 +485,15 @@
     full[other, :] = fin_in[...].astype(jnp.float32)
     full[own, :] = fin[...]
     total = full[...].T
-    out_ref[core] = total[:cols]
-    out_ref[1 - core] = total[cols:]
+    out_ref[core] = total[:cols] * factor
+    out_ref[1 - core] = total[cols:] * factor
     for s in range(slots):
         for j in range(owners - 1):
             give(s, j).wait()
 
 
 def fused_step(
-    next_ids, next_lengths, slot_of_table, tables, cross_input, cotangent, up_weight, down_weight, maxlen
+    next_ids, next_lengths, slot_of_table, tables, cross_input, cotangent, up_weight, down_weight, maxlen, factor
 ):
     groups, owners = lax.axis_size("grp"), lax.axis_size("tbl")
     slots, rows, width = tables.shape
@@ -502,7 +503,7 @@
     half = (high // 2 + 15) // 16 * 16
     sems = pltpu.SemaphoreType.DMA
     bf16, f32 = jnp.bfloat16, jnp.float32
-    any_space = pl.BlockSpec(memory_space=pl.ANY)
+    in_hbm = pl.BlockSpec(memory_space=pltpu.HBM)
     idx_shape = (owners, next_ids.shape[1] // owners, batch)
     vmem = pl.BlockSpec(memory_space=pltpu.VMEM)
     landing = [
@@ -511,12 +512,12 @@
         for i in range(4)
     ]
     return pl.pallas_call(
-        functools.partial(step_kernel, maxlen),
+        functools.partial(step_kernel, maxlen, factor),
         out_shape=(
-            jax.ShapeDtypeStruct((owners, slots, batch, width), bf16),
-            jax.ShapeDtypeStruct((2, rank // owners, high), f32),
+            pltpu.VMEM((owners, slots, batch, width), bf16),
+            pltpu.VMEM((2, rank // owners, high), f32),
         ),
-        in_specs=[any_space] * 8,
+        in_specs=[in_hbm] * 8,
         out_specs=(vmem, vmem),
         scratch_shapes=[
             pltpu.VMEM(next_ids.shape[::-1], jnp.int32),
@@ -562,38 +563,60 @@
         ),
         name="fused_step",
     )(
-        next_ids.T,
-        next_lengths.T,
-        slot_of_table[None, :],
-        tables,
-        cross_input,
-        cotangent,
-        up_weight,
-        down_weight,
-    )
-
-
-def finish_kernel(factor, slot_ref, got_ref, sum_ref, emb_ref, grad_up_ref, grad_down_ref):
+        *(
+            pltpu.with_memory_space_constraint(a, pltpu.HBM)
+            for a in (
+                next_ids.T,
+                next_lengths.T,
+                slot_of_table[None, :],
+                tables,
+                cross_input,
+                cotangent,
+                up_weight,
+                down_weight,
+            )
+        )
+    )
+
+
+def finish_kernel(slot_ref, got_ref, sum_ref, emb_ref, grad_up_ref, grad_down_ref, sem):
     slots, _, width = got_ref.shape[1:]
-    for f in range(slot_ref.shape[0]):
+    feats = slot_ref.shape[0]
+    copies = [
+        pltpu.make_async_copy(sum_ref.at[0], grad_up_ref, sem.at[feats]),
+        pltpu.make_async_copy(sum_ref.at[1], grad_down_ref, sem.at[feats + 1]),
+    ]
+    for f in range(feats):
         s = slot_ref[f]
-        emb_ref[:, f * width : (f + 1) * width] = got_ref[lax.div(s, slots), lax.rem(s, slots)]
-    grad_up_ref[...] = sum_ref[0] * factor
-    grad_down_ref[...] = sum_ref[1] * factor
-
-
-def finish(slot_of_table, got, sums, factor):
+        copies.append(
+            pltpu.make_async_copy(
+                got_ref.at[lax.div(s, slots), lax.rem(s, slots)],
+                emb_ref.at[:, pl.ds(f * width, width)],
+                sem.at[f],
+            )
+        )
+    for copy in copies:
+        copy.start()
+    for copy in copies:
+        copy.wait()
+
+
+def finish(slot_of_table, got, sums):
     _, _, batch, width = got.shape
-    vmem = pl.BlockSpec(memory_space=pltpu.VMEM)
+    feats = slot_of_table.shape[0]
+    in_hbm = pl.BlockSpec(memory_space=pltpu.HBM)
+    any_space = pl.BlockSpec(memory_space=pl.ANY)
     return pl.pallas_call(
-        functools.partial(finish_kernel, factor),
+        finish_kernel,
         out_shape=(
-            jax.ShapeDtypeStruct((batch, slot_of_table.shape[0] * width), jnp.bfloat16),
+            jax.ShapeDtypeStruct((batch, feats * width), jnp.bfloat16),
             jax.ShapeDtypeStruct(sums.shape[1:], jnp.float32),
             jax.ShapeDtypeStruct(sums.shape[1:], jnp.float32),
         ),
-        in_specs=[pl.BlockSpec(memory_space=pltpu.SMEM), vmem, vmem],
-        out_specs=(vmem, vmem, vmem),
+        in_specs=[pl.BlockSpec(memory_space=pltpu.SMEM), any_space, any_space],
+        out_specs=(in_hbm, in_hbm, in_hbm),
+        scratch_shapes=[pltpu.SemaphoreType.DMA((feats + 2,))],
+        compiler_params=pltpu.CompilerParams(vmem_limit_bytes=1 << 20),
         name="finish",
     )(slot_of_table, got, sums)
 
@@ -631,9 +654,9 @@
     )
     if not fits:
         return plain(*args)
-    got, sums = fused_step(*args, maxlen)
     factor = 1.0 / math.sqrt(batch * groups * owners)
-    next_embedded, grad_up, grad_down = finish(slot_of_table, got, sums, factor)
+    got, sums = fused_step(*args, maxlen, factor)
+    next_embedded, grad_up, grad_down = finish(slot_of_table, got, sums)
     return next_embedded, grad_up, grad_down.T
 
 

time: 48.6 us -> 40 us (0.82)
  local copies, waits for them, and re-layouts: 7.72 us -> 0.01 us
  Pallas kernels: 39.8 us -> 39.2 us
    unnamed x16 -> x2, local copies, waits for them, and re-layouts: 7.72 us -> 0.01 us
    pallas_call x2, Pallas kernels: 39.8 us -> 39.2 us  [the longest x1 37.4 us: fused_step(): pl.pallas_call(functools.partial(step_kernel, maxlen, factor), out_shape=...]
where the time goes in v3:
time: 40 us; the launch traced here: 39.9 us
  Pallas kernels  39.2 us (98%)
  between operations  0.66 us (2%)
    pallas_call x1, Pallas kernels, fused_step(): pl.pallas_call(functools.partial(step_kernel, maxlen, factor), out_shape=...  37.4 us
    pallas_call x1, Pallas kernels, finish(): pl.pallas_call(finish_kernel, out_shape=(jax.ShapeDtypeStruct((batch, fea...  1.75 us

profile of v3, /device:TPU:0, one launch (start us, length us, event | category | flops | bytes accessed | tf_op | source)
XLA Modules:
  0.0 39.9 jit_solution(7507550273249275691)
XLA Ops:
  0.6 0.0 copy-start
  0.6 37.4 %fused_step.1 = (bf16[4,7,128,128]{3,2,1,0:T(8,128)(2,1)S(1)}, f32[2,64,432]{2,1,0:T(8,128)S(1)}) custom-call(s32[224,128]{1,0:T(8,128)} %bitcast.5, s32[26,128]{1,0:T(8,128)} %bitcast.6, s32[1,26]{1,0:T(1,128)} %bitcast.4, bf16[7,6144,128]{2,1,0:T(8,128)(2,1)} %tab_ref.1, bf16[128,3456]{1,0:T(8,128)(2,1)} %x_hbm.1, bf16[128,3456]{1,0:T(8,128)(2,1)} %ct_hbm.1, ...), custom_call_target="tpu_custom_call" | custom-call | tf_op jit(solution)/shard_map/fused_step/pallas_call | solution.py:514
  38.1 0.0 copy-done
  38.1 1.8 %finish.1 = (bf16[128,3328]{1,0:T(8,128)(2,1)}, f32[64,432]{1,0:T(8,128)}, f32[64,432]{1,0:T(8,128)}) custom-call(s32[26]{0:T(128)S(1)} %copy-done, bf16[4,7,128,128]{3,2,1,0:T(8,128)(2,1)S(1)} %get-tuple-element.8.got_ref, f32[2,64,432]{2,1,0:T(8,128)S(1)} %get-tuple-element.9.sum_ref), custom_call_target="tpu_custom_call" | custom-call | tf_op jit(solution)/shard_map/finish/pallas_call | solution.py:609
Async XLA Ops:
  0.6 37.5 %copy-start = (s32[26]{0:T(128)S(1)}, s32[26]{0:T(128)}, u32[]{:S(2)}) copy-start(s32[26]{0:T(128)} %slot_ref.1) | copy-start | bytes 316

commit v4 on v3

--- a/solution.py
+++ b/solution.py
@@ -165,11 +165,12 @@
     ct_hbm,
     up_hbm,
     down_hbm,
-    got,
+    emb_ref,
     out_ref,
     ids_ref,
     len_ref,
     slot_ref,
+    slot_s,
     x_ref,
     ct_ref,
     up_ref,
@@ -185,16 +186,15 @@
     idx_ref,
     idx_in,
     idx_s,
+    rise,
     part,
-    fin,
-    fin_out,
-    fin_in,
     full,
     stage,
     wide_even,
     wide_odd,
     acc,
     pooled,
+    got,
     tab_sem,
     smem_sem,
     idx_sem,
@@ -245,17 +245,21 @@
                 (len_hbm, len_ref),
                 (slot_hbm, slot_ref),
                 (x_hbm, x_ref),
+                (ct_hbm, ct_ref),
                 (down_hbm, down_ref),
-                (ct_hbm, ct_ref),
                 (up_hbm, up_ref),
+                (slot_hbm, slot_s),
             )
         )
     ]
     for copy in loads:
         copy.start()
     fetch(0).start()
+    fetch(1).start()
     barrier = pltpu.get_barrier_semaphore()
+    beside = {d: (a, b + 1 - 2 * core) for d, (a, b) in across.items()}
     near = [(g, (t + d) % owners) for d in range(1, owners)] + [across[d] for d in "vux"]
+    near += [beside[d] for d in "vux" if any(order[3] == d for order, _ in PLAN)]
     for device in near:
         pl.semaphore_signal(
             barrier, inc=1, device_id=device, device_id_type=pl.DeviceIdType.MESH
@@ -279,15 +283,6 @@
         for n in range(depth // LANES):
             at = slice(n * LANES, (n + 1) * LANES)
             dst[at, :] = src[:, at].T
-
-    loads[3].wait()
-    turn(x_ref, xt)
-    loads[4].wait()
-    low_ref[...] = jnp.dot(
-        x_ref[...], down_ref[...], preferred_element_type=jnp.float32
-    ).astype(jnp.bfloat16)
-
-    pl.semaphore_wait(barrier, len(near))
 
     ids_out = [
         send(idx_ref.at[(t + d) % owners], idx_in.at[t], idx_sem, d - 1, (g, (t + d) % owners))
@@ -309,20 +304,27 @@
     x_out, dz_out = lend(xt, x_in, 0), lend(dzt, dz_in, groups)
     low_out = send(low_ref, low_in, mate_sem, 2 * groups, mate)
     dlow_out = send(dlow_ref, dlow_in, mate_sem, 2 * groups + 1, mate)
-    for copy in ids_out + x_out + [low_out]:
+    for wide in (wide_even, wide_odd):
+        wide[pl.ds(rows, 8), :] = jnp.zeros((8, width), jnp.float32)
+    loads[3].wait()
+    turn(x_ref, xt)
+    pl.semaphore_wait(barrier, len(near))
+    for copy in ids_out + x_out:
         copy.start()
-
-    loads[5].wait()
+    loads[4].wait()
     ct_ref[...] = (ct_ref[...].astype(jnp.float32) * x_ref[...].astype(jnp.float32)).astype(
         jnp.bfloat16
     )
     turn(ct_ref, dzt)
     for copy in dz_out:
         copy.start()
+    loads[5].wait()
+    low_ref[...] = jnp.dot(
+        x_ref[...], down_ref[...], preferred_element_type=jnp.float32
+    ).astype(jnp.bfloat16)
+    low_out.start()
     loads[6].wait()
-    dlow = lax.dot_general(
-        ct_ref[...], up_ref[...], (((1,), (1,)), ((), ())), preferred_element_type=jnp.float32
-    ).astype(jnp.bfloat16)
+    dlow = jnp.dot(up_ref[...], dzt[...], preferred_element_type=jnp.float32).astype(jnp.bfloat16).T
     swap = [n + 1 - 2 * (n % 2) for n in range(owners)]
     dlow_ref[...] = jnp.concatenate([dlow[:, n * cols : (n + 1) * cols] for n in swap], axis=1)
     dlow_out.start()
@@ -332,18 +334,11 @@
     def widen(s, at):
         wides[s % 2][at, :] = stage[s % 2, at, :].astype(jnp.float32)
 
-    for wide in wides:
-        wide[pl.ds(rows, 8), :] = jnp.zeros((8, width), jnp.float32)
-    fetch(1).start()
     fetch(0).wait()
 
     @pl.loop(0, rows // chunk)
     def _(c):
         widen(0, pl.ds(pl.multiple_of(c * chunk, chunk), chunk))
-
-    for copy in ids_out:
-        copy.wait()
-    idx_in[t] = idx_ref[t]
 
     def peer(j):
         return (t // 2 + 1 - j // 2) % 2 * 2 + (t + (j + 1) // 2) % 2
@@ -359,31 +354,32 @@
         ]
         for s in range(slots)
     ]
+    for copy in ids_out:
+        copy.wait()
+    idx_in[t] = idx_ref[t]
     for copies in got_ids:
         for copy in copies:
             copy.start()
-
-    for copy in x_out + dz_out + [low_out, dlow_out]:
+    for copy in dz_out + [low_out]:
         copy.wait()
+    rises = [
+        pl.ds(pl.multiple_of(b * high + core * (high - half), 16), half) for b in range(groups)
+    ]
     low_two = jnp.concatenate([low_ref[...], low_in[...]], axis=0)
+    for b in range(groups):
+        both = jnp.concatenate([dzt[rises[b], :], dz_in[b]], axis=1)
+        rise[b] = jnp.dot(both, low_two, preferred_element_type=jnp.float32).astype(jnp.bfloat16)
+    for copy in x_out + [dlow_out]:
+        copy.wait()
     dlow_two = jnp.concatenate([dlow_ref[...], dlow_in[...]], axis=0)
     left = lax.broadcasted_iota(jnp.int32, (half, LANES), 1) < cols
     for b in range(groups):
-        at = pl.ds(pl.multiple_of(b * high + core * (high - half), 16), half)
-        up = jnp.dot(
-            jnp.concatenate([dzt[at, :], dz_in[b]], axis=1),
-            low_two,
-            preferred_element_type=jnp.float32,
-        )
-        down = jnp.dot(
-            jnp.concatenate([xt[at, :], x_in[b]], axis=1),
-            dlow_two,
-            preferred_element_type=jnp.float32,
-        )
+        both = jnp.concatenate([xt[rises[b], :], x_in[b]], axis=1)
+        down = jnp.dot(both, dlow_two, preferred_element_type=jnp.float32).astype(jnp.bfloat16)
         for y in range(2):
-            u, d = up[:, y * LANES : (y + 1) * LANES], down[:, y * LANES : (y + 1) * LANES]
-            part[y, 0, b // 4, b // 2 % 2, b % 2] = jnp.where(left, u, d).astype(jnp.bfloat16)
-            part[y, 1, b // 4, b // 2 % 2, b % 2] = jnp.where(left, d, u).astype(jnp.bfloat16)
+            u, d = rise[b, :, y * LANES : (y + 1) * LANES], down[:, y * LANES : (y + 1) * LANES]
+            part[y, 0, b // 4, b // 2 % 2, b % 2] = jnp.where(left, u, d)
+            part[y, 1, b // 4, b // 2 % 2, b % 2] = jnp.where(left, d, u)
 
     begins = [sum(n for _, n in PLAN[:k]) * half // 14 for k in range(len(PLAN) + 1)]
 
@@ -399,33 +395,60 @@
             part.at[place_of(k, held)], landing[4 * k + i], class_sem, 4 * k + i, across[order[i]]
         )
 
-    def hand(k):
-        span = pl.ds(begins[k], begins[k + 1] - begins[k])
-        return send(fin_out.at[span], fin_in.at[span], fin_sem, k, mate)
+    def last(k):
+        order = PLAN[k][0]
+        d = order[3]
+        held = {e: at_axis[e] for e in order}
+        there, here = held | {d: 1 - at_axis[d]}, held
+        return [
+            send(
+                part.at[place_of(k, there | {"c": core})],
+                landing[4 * k + 3].at[0],
+                class_sem,
+                4 * k + 3,
+                across[d],
+            ),
+            send(
+                part.at[place_of(k, there | {"c": 1 - core})],
+                landing[4 * k + 3].at[1],
+                fin_sem,
+                2 * k,
+                beside[d],
+            ),
+            send(
+                part.at[place_of(k, here | {"c": 1 - core})],
+                landing[4 * k + 3].at[2],
+                fin_sem,
+                2 * k + 1,
+                mate,
+            ),
+        ]
 
     def take(k, i):
-        exchange(k, i).wait()
         order, came = PLAN[k][0], landing[4 * k + i]
         held = {d: at_axis[d] for d in order[: i + 1]}
-        span = pl.ds(begins[k], begins[k + 1] - begins[k])
         if i == 3:
-            for c, keep in ((1 - core, False), (core, True)):
-                total = part[place_of(k, held | {"c": c})].astype(jnp.float32) + came[c].astype(
-                    jnp.float32
-                )
-                if keep:
-                    fin[span, :] = total
-                else:
-                    fin_out[span, :] = total.astype(jnp.bfloat16)
-                    hand(k).start()
+            for copy in last(k):
+                copy.wait()
+            size = begins[k + 1] - begins[k]
+            other = pl.ds(pl.multiple_of((1 - core) * (high - half) + begins[k], 16), size)
+            own = pl.ds(pl.multiple_of(core * (high - half) + begins[k], 16), size)
+            mine = part[place_of(k, held | {"c": core})].astype(jnp.float32)
+            full[other, :] = came[1].astype(jnp.float32) + came[2].astype(jnp.float32)
+            full[own, :] = mine + came[0].astype(jnp.float32)
             return
+        exchange(k, i).wait()
         free = [d for d in "ycvux" if d not in held]
         for pick in itertools.product(range(2), repeat=len(free)):
             at = place_of(k, held | dict(zip(free, pick)))
             part[at] = (part[at].astype(jnp.float32) + came[pick].astype(jnp.float32)).astype(
                 jnp.bfloat16
             )
-        exchange(k, i + 1).start()
+        if i == 2:
+            for copy in last(k):
+                copy.start()
+        else:
+            exchange(k, i + 1).start()
 
     for k in range(len(PLAN)):
         if k not in dict(LATE):
@@ -475,21 +498,20 @@
 
         got[t, s] = pooled[owners - 1, s]
 
-    for now, k, i in POLLS:
-        if now >= slots * owners:
-            take(k, i)
-    for k in range(len(PLAN)):
-        hand(k).wait()
-    other = pl.ds(pl.multiple_of((1 - core) * (high - half), 16), half)
-    own = pl.ds(pl.multiple_of(core * (high - half), 16), half)
-    full[other, :] = fin_in[...].astype(jnp.float32)
-    full[own, :] = fin[...]
+    tail = [(k, i) for now, k, i in POLLS if now >= slots * owners]
+    for n, (k, i) in enumerate(tail):
+        if all(i == 3 for _, i in tail[n:]) and tail[n - 1][1] < 3:
+            for s in range(slots):
+                for j in range(owners - 1):
+                    give(s, j).wait()
+            loads[7].wait()
+            for f in range(feats):
+                s = slot_s[0, f]
+                emb_ref[:, f * width : (f + 1) * width] = got[lax.div(s, slots), lax.rem(s, slots)]
+        take(k, i)
     total = full[...].T
     out_ref[core] = total[:cols] * factor
     out_ref[1 - core] = total[cols:] * factor
-    for s in range(slots):
-        for j in range(owners - 1):
-            give(s, j).wait()
 
 
 def fused_step(
@@ -507,14 +529,14 @@
     idx_shape = (owners, next_ids.shape[1] // owners, batch)
     vmem = pl.BlockSpec(memory_space=pltpu.VMEM)
     landing = [
-        pltpu.VMEM((2,) * (4 - i) + (n * half // 14, LANES), bf16)
+        pltpu.VMEM(((2,) * (4 - i) if i < 3 else (3,)) + (n * half // 14, LANES), bf16)
         for _, n in PLAN
         for i in range(4)
     ]
     return pl.pallas_call(
         functools.partial(step_kernel, maxlen, factor),
         out_shape=(
-            pltpu.VMEM((owners, slots, batch, width), bf16),
+            pltpu.VMEM((batch, slot_of_table.shape[0] * width), bf16),
             pltpu.VMEM((2, rank // owners, high), f32),
         ),
         in_specs=[in_hbm] * 8,
@@ -523,6 +545,7 @@
             pltpu.VMEM(next_ids.shape[::-1], jnp.int32),
             pltpu.VMEM(next_lengths.shape[::-1], jnp.int32),
             pltpu.VMEM((1, slot_of_table.shape[0]), jnp.int32),
+            pltpu.SMEM((1, slot_of_table.shape[0]), jnp.int32),
             pltpu.VMEM(cross_input.shape, bf16),
             pltpu.VMEM(cotangent.shape, bf16),
             pltpu.VMEM(up_weight.shape, bf16),
@@ -538,24 +561,23 @@
             pltpu.VMEM(idx_shape, jnp.int32),
             pltpu.VMEM(idx_shape, jnp.int32),
             pltpu.SMEM((slots, owners, maxlen, batch), jnp.int32),
+            pltpu.VMEM((groups, half, rank), bf16),
             pltpu.VMEM((2, 2, 2, 2, 2, half, LANES), bf16),
-            pltpu.VMEM((half, LANES), f32),
-            pltpu.VMEM((half, LANES), bf16),
-            pltpu.VMEM((half, LANES), bf16),
             pltpu.VMEM((high, LANES), f32),
             pltpu.VMEM((2, rows, width), bf16),
             pltpu.VMEM((rows + 8, width), f32),
             pltpu.VMEM((rows + 8, width), f32),
             pltpu.VMEM((batch, width), f32),
             pltpu.VMEM((owners, slots, batch, width), bf16),
+            pltpu.VMEM((owners, slots, batch, width), bf16),
             sems((2,)),
             sems((slots * owners,)),
             sems((2, owners - 1)),
             sems((2, 2 * groups + 2)),
             sems((2, 4 * len(PLAN))),
-            sems((2, len(PLAN))),
+            sems((2, 2 * len(PLAN))),
             sems((2, slots * (owners - 1))),
-            sems((7,)),
+            sems((8,)),
         ]
         + landing,
         compiler_params=pltpu.CompilerParams(
@@ -579,46 +601,35 @@
     )
 
 
-def finish_kernel(slot_ref, got_ref, sum_ref, emb_ref, grad_up_ref, grad_down_ref, sem):
-    slots, _, width = got_ref.shape[1:]
-    feats = slot_ref.shape[0]
+def finish_kernel(emb_in, sum_in, emb_ref, grad_up_ref, grad_down_ref, sem):
     copies = [
-        pltpu.make_async_copy(sum_ref.at[0], grad_up_ref, sem.at[feats]),
-        pltpu.make_async_copy(sum_ref.at[1], grad_down_ref, sem.at[feats + 1]),
+        pltpu.make_async_copy(a, b, sem.at[n])
+        for n, (a, b) in enumerate(
+            ((emb_in, emb_ref), (sum_in.at[0], grad_up_ref), (sum_in.at[1], grad_down_ref))
+        )
     ]
-    for f in range(feats):
-        s = slot_ref[f]
-        copies.append(
-            pltpu.make_async_copy(
-                got_ref.at[lax.div(s, slots), lax.rem(s, slots)],
-                emb_ref.at[:, pl.ds(f * width, width)],
-                sem.at[f],
-            )
-        )
     for copy in copies:
         copy.start()
     for copy in copies:
         copy.wait()
 
 
-def finish(slot_of_table, got, sums):
-    _, _, batch, width = got.shape
-    feats = slot_of_table.shape[0]
+def finish(emb, sums):
     in_hbm = pl.BlockSpec(memory_space=pltpu.HBM)
     any_space = pl.BlockSpec(memory_space=pl.ANY)
     return pl.pallas_call(
         finish_kernel,
         out_shape=(
-            jax.ShapeDtypeStruct((batch, feats * width), jnp.bfloat16),
+            jax.ShapeDtypeStruct(emb.shape, emb.dtype),
             jax.ShapeDtypeStruct(sums.shape[1:], jnp.float32),
             jax.ShapeDtypeStruct(sums.shape[1:], jnp.float32),
         ),
-        in_specs=[pl.BlockSpec(memory_space=pltpu.SMEM), any_space, any_space],
+        in_specs=[any_space, any_space],
         out_specs=(in_hbm, in_hbm, in_hbm),
-        scratch_shapes=[pltpu.SemaphoreType.DMA((feats + 2,))],
+        scratch_shapes=[pltpu.SemaphoreType.DMA((3,))],
         compiler_params=pltpu.CompilerParams(vmem_limit_bytes=1 << 20),
         name="finish",
-    )(slot_of_table, got, sums)
+    )(emb, sums)
 
 
 def on_device(
@@ -655,8 +666,7 @@
     if not fits:
         return plain(*args)
     factor = 1.0 / math.sqrt(batch * groups * owners)
-    got, sums = fused_step(*args, maxlen, factor)
-    next_embedded, grad_up, grad_down = finish(slot_of_table, got, sums)
+    next_embedded, grad_up, grad_down = finish(*fused_step(*args, maxlen, factor))
     return next_embedded, grad_up, grad_down.T
 
 

time: 40 us -> 37.3 us (0.932)
  Pallas kernels: 39.2 us -> 36.5 us
    pallas_call x1, Pallas kernels: 37.4 us -> 35.5 us  [fused_step(): pl.pallas_call(functools.partial(step_kernel, maxlen, factor), out_shape=...]
    pallas_call x1, Pallas kernels: 1.75 us -> 1.01 us  [finish(): pl.pallas_call(finish_kernel, out_shape=(jax.ShapeDtypeStruct(emb.shape,...]
where the time goes in v4:
time: 37.3 us; the launch traced here: 37.2 us
  Pallas kernels  36.5 us (98%)
  between operations  0.64 us (2%)
    pallas_call x1, Pallas kernels, fused_step(): pl.pallas_call(functools.partial(step_kernel, maxlen, factor), out_shape=...  35.5 us
    pallas_call x1, Pallas kernels, finish(): pl.pallas_call(finish_kernel, out_shape=(jax.ShapeDtypeStruct(emb.shape,...  1.01 us

profile of v4, /device:TPU:0, one launch (start us, length us, event | category | flops | bytes accessed | tf_op | source)
XLA Modules:
  0.0 37.2 jit_solution(11752536033927540657)
XLA Ops:
  0.6 35.5 %fused_step.1 = (bf16[128,3328]{1,0:T(8,128)(2,1)S(1)}, f32[2,64,432]{2,1,0:T(8,128)S(1)}) custom-call(s32[224,128]{1,0:T(8,128)} %bitcast.4, s32[26,128]{1,0:T(8,128)} %bitcast.5, s32[1,26]{1,0:T(1,128)} %bitcast.6, bf16[7,6144,128]{2,1,0:T(8,128)(2,1)} %tab_ref.1, bf16[128,3456]{1,0:T(8,128)(2,1)} %x_hbm.1, bf16[128,3456]{1,0:T(8,128)(2,1)} %ct_hbm.1, ...), custom_call_target="tpu_custom_call" | custom-call | tf_op jit(solution)/shard_map/fused_step/pallas_call | solution.py:536
  36.1 1.0 %finish.1 = (bf16[128,3328]{1,0:T(8,128)(2,1)}, f32[64,432]{1,0:T(8,128)}, f32[64,432]{1,0:T(8,128)}) custom-call(bf16[128,3328]{1,0:T(8,128)(2,1)S(1)} %get-tuple-element.8.emb_in, f32[2,64,432]{2,1,0:T(8,128)S(1)} %get-tuple-element.9.sum_in), custom_call_target="tpu_custom_call" | custom-call | tf_op jit(solution)/shard_map/finish/pallas_call | solution.py:620

commit v5 on v4

--- a/solution.py
+++ b/solution.py
@@ -149,9 +149,14 @@
     return (next_embedded, grad_up, grad_down)
 
 
-PLAN = (("uxyv", 5), ("yuxv", 3), ("xyuv", 2), ("xuvy", 4))
-POLLS = ((12, 3, 0), (13, 0, 0), (15, 2, 0), (15, 1, 0), (21, 3, 1), (22, 2, 1), (23, 1, 1), (23, 0, 1), (28, 1, 2), (28, 2, 2), (28, 0, 2), (28, 3, 2), (28, 2, 3), (28, 3, 3), (28, 1, 3), (28, 0, 3))
-LATE = ((2, 7),)
+PLAN = (("uxy", "v", 3), ("xy", "vu", 2), ("vux", "y", 3), ("xuv", "y", 4), ("yxu", "v", 2))
+POLLS = ((11, 3, 0), (13, 4, 0), (15, 0, 0), (16, 2, 0), (18, 1, 0), (19, 4, 1), (19, 3, 1), (22, 0, 1), (24, 1, 1), (25, 4, 2), (25, 2, 1), (28, 0, 2), (28, 3, 2), (28, 2, 2), (28, 4, 3), (28, 1, 2), (28, 3, 3), (28, 0, 3), (28, 2, 3))
+LATE = ((1, 8), (4, 1))
+SORT = 3
+
+
+def flips(final):
+    return ["".join(p) for n in range(1, len(final) + 1) for p in itertools.combinations(final, n)]
 
 
 def step_kernel(
@@ -199,8 +204,7 @@
     smem_sem,
     idx_sem,
     mate_sem,
-    class_sem,
-    fin_sem,
+    step_sem,
     pool_sem,
     load_sem,
     *landing,
@@ -216,24 +220,28 @@
     g, t = lax.axis_index("grp"), lax.axis_index("tbl")
     core = t % 2
     at_axis = {"y": t // 2, "v": g // 4, "u": g // 2 % 2, "x": g % 2}
-    mate = (g, t + 1 - 2 * core)
-    across = {
-        "y": (g, (t + 2) % owners),
-        "v": ((g + 4) % groups, t),
-        "u": (g + 2 - 4 * at_axis["u"], t),
-        "x": (g + 1 - 2 * at_axis["x"], t),
-    }
+
+    def device(flip, turned=False):
+        at = {d: 1 - v if d in flip else v for d, v in at_axis.items()}
+        c = 1 - core if turned else core
+        return at["v"] * 4 + at["u"] * 2 + at["x"], at["y"] * 2 + c
+
+    mate = device("", True)
+    meets = {("y", False), ("y", True), ("", True)}
+    for head, final, _ in PLAN:
+        meets |= {(d, False) for d in head}
+        meets |= {(flip, c) for flip in flips(final) for c in (False, True)}
 
     def fetch(s):
         return pltpu.make_async_copy(tab_ref.at[s], stage.at[s % 2], tab_sem.at[s % 2])
 
-    def send(src, dst, sems, n, device):
+    def send(src, dst, out_sem, in_sem, who):
         return pltpu.make_async_remote_copy(
             src_ref=src,
             dst_ref=dst,
-            send_sem=sems.at[0, n],
-            recv_sem=sems.at[1, n],
-            device_id=device,
+            send_sem=out_sem,
+            recv_sem=in_sem,
+            device_id=who,
             device_id_type=pl.DeviceIdType.MESH,
         )
 
@@ -257,13 +265,9 @@
     fetch(0).start()
     fetch(1).start()
     barrier = pltpu.get_barrier_semaphore()
-    beside = {d: (a, b + 1 - 2 * core) for d, (a, b) in across.items()}
-    near = [(g, (t + d) % owners) for d in range(1, owners)] + [across[d] for d in "vux"]
-    near += [beside[d] for d in "vux" if any(order[3] == d for order, _ in PLAN)]
-    for device in near:
-        pl.semaphore_signal(
-            barrier, inc=1, device_id=device, device_id_type=pl.DeviceIdType.MESH
-        )
+    near = [device(*who) for who in sorted(meets)]
+    for who in near:
+        pl.semaphore_signal(barrier, inc=1, device_id=who, device_id_type=pl.DeviceIdType.MESH)
 
     for copy in loads[:3]:
         copy.wait()
@@ -281,50 +285,63 @@
 
     def turn(src, dst):
         for n in range(depth // LANES):
-            at = slice(n * LANES, (n + 1) * LANES)
-            dst[at, :] = src[:, at].T
+            turned = src[:, n * LANES : (n + 1) * LANES].T
+            begin, stop = n * LANES, (n + 1) * LANES
+            while begin < stop:
+                b, row = divmod(begin, high)
+                size = min(high - row, stop - begin)
+                dst[b, row : row + size] = turned[begin - n * LANES : begin - n * LANES + size]
+                begin += size
+
+    def peer(j):
+        return (t // 2 + 1 - j // 2) % 2 * 2 + (t + (j + 1) // 2) % 2
 
     ids_out = [
-        send(idx_ref.at[(t + d) % owners], idx_in.at[t], idx_sem, d - 1, (g, (t + d) % owners))
-        for d in range(1, owners)
+        send(idx_ref.at[peer(j)], idx_in.at[j], idx_sem.at[0], idx_sem.at[1], (g, peer(j)))
+        for j in range(owners - 1)
     ]
-
-    def lend(src, dst, n):
-        return [
-            send(
-                src.at[pl.ds(pl.multiple_of(b * high + (1 - core) * (high - half), 16), half)],
-                dst.at[b],
-                mate_sem,
-                n + b,
-                mate,
+    ids_all = send(
+        idx_in.at[pl.ds(0, owners - 1)],
+        idx_in.at[pl.ds(0, owners - 1)],
+        idx_sem.at[0],
+        idx_sem.at[1],
+        mate,
+    )
+    lent = pl.ds(pl.multiple_of((1 - core) * (high - half), 16), half)
+    x_out, dz_out, low_out, dlow_out = (
+        send(src, dst, mate_sem.at[0, n], mate_sem.at[1, n], mate)
+        for n, (src, dst) in enumerate(
+            (
+                (xt.at[:, lent], x_in),
+                (dzt.at[:, lent], dz_in),
+                (low_ref, low_in),
+                (dlow_ref, dlow_in),
             )
-            for b in range(groups)
-        ]
-
-    x_out, dz_out = lend(xt, x_in, 0), lend(dzt, dz_in, groups)
-    low_out = send(low_ref, low_in, mate_sem, 2 * groups, mate)
-    dlow_out = send(dlow_ref, dlow_in, mate_sem, 2 * groups + 1, mate)
+        )
+    )
     for wide in (wide_even, wide_odd):
         wide[pl.ds(rows, 8), :] = jnp.zeros((8, width), jnp.float32)
     loads[3].wait()
     turn(x_ref, xt)
     pl.semaphore_wait(barrier, len(near))
-    for copy in ids_out + x_out:
+    for copy in ids_out + [x_out]:
         copy.start()
     loads[4].wait()
     ct_ref[...] = (ct_ref[...].astype(jnp.float32) * x_ref[...].astype(jnp.float32)).astype(
         jnp.bfloat16
     )
     turn(ct_ref, dzt)
-    for copy in dz_out:
-        copy.start()
+    dz_out.start()
     loads[5].wait()
     low_ref[...] = jnp.dot(
         x_ref[...], down_ref[...], preferred_element_type=jnp.float32
     ).astype(jnp.bfloat16)
     low_out.start()
     loads[6].wait()
-    dlow = jnp.dot(up_ref[...], dzt[...], preferred_element_type=jnp.float32).astype(jnp.bfloat16).T
+    dlow = jnp.dot(
+        up_ref[...], dzt[...].reshape(depth, batch), preferred_element_type=jnp.float32
+    )
+    dlow = dlow.astype(jnp.bfloat16).T
     swap = [n + 1 - 2 * (n % 2) for n in range(owners)]
     dlow_ref[...] = jnp.concatenate([dlow[:, n * cols : (n + 1) * cols] for n in swap], axis=1)
     dlow_out.start()
@@ -340,127 +357,115 @@
     def _(c):
         widen(0, pl.ds(pl.multiple_of(c * chunk, chunk), chunk))
 
-    def peer(j):
-        return (t // 2 + 1 - j // 2) % 2 * 2 + (t + (j + 1) // 2) % 2
-
+    ids_all.wait()
+    idx_in[owners - 1] = idx_ref[t]
     got_ids = [
-        [
-            pltpu.make_async_copy(
-                idx_in.at[peer(j), pl.ds(s * maxlen, maxlen)],
-                idx_s.at[s, j],
-                smem_sem.at[s * owners + j],
-            )
-            for j in range(owners)
-        ]
+        pltpu.make_async_copy(
+            idx_in.at[:, pl.ds(s * maxlen, maxlen)], idx_s.at[s], smem_sem.at[min(s, 2)]
+        )
         for s in range(slots)
     ]
-    for copy in ids_out:
-        copy.wait()
-    idx_in[t] = idx_ref[t]
-    for copies in got_ids:
-        for copy in copies:
-            copy.start()
-    for copy in dz_out + [low_out]:
-        copy.wait()
-    rises = [
-        pl.ds(pl.multiple_of(b * high + core * (high - half), 16), half) for b in range(groups)
-    ]
+    for copy in got_ids:
+        copy.start()
+    dz_out.wait()
+    low_out.wait()
+    kept = pl.ds(pl.multiple_of(core * (high - half), 16), half)
     low_two = jnp.concatenate([low_ref[...], low_in[...]], axis=0)
     for b in range(groups):
-        both = jnp.concatenate([dzt[rises[b], :], dz_in[b]], axis=1)
+        both = jnp.concatenate([dzt[b, kept], dz_in[b]], axis=1)
         rise[b] = jnp.dot(both, low_two, preferred_element_type=jnp.float32).astype(jnp.bfloat16)
-    for copy in x_out + [dlow_out]:
-        copy.wait()
+    x_out.wait()
+    dlow_out.wait()
     dlow_two = jnp.concatenate([dlow_ref[...], dlow_in[...]], axis=0)
     left = lax.broadcasted_iota(jnp.int32, (half, LANES), 1) < cols
     for b in range(groups):
-        both = jnp.concatenate([xt[rises[b], :], x_in[b]], axis=1)
+        both = jnp.concatenate([xt[b, kept], x_in[b]], axis=1)
         down = jnp.dot(both, dlow_two, preferred_element_type=jnp.float32).astype(jnp.bfloat16)
         for y in range(2):
             u, d = rise[b, :, y * LANES : (y + 1) * LANES], down[:, y * LANES : (y + 1) * LANES]
             part[y, 0, b // 4, b // 2 % 2, b % 2] = jnp.where(left, u, d)
             part[y, 1, b // 4, b // 2 % 2, b % 2] = jnp.where(left, d, u)
 
-    begins = [sum(n for _, n in PLAN[:k]) * half // 14 for k in range(len(PLAN) + 1)]
+    sizes = [n * half // 14 for _, _, n in PLAN]
+    begins = [sum(sizes[:k]) for k in range(len(PLAN))]
+    steps = [len(head) + 1 for head, _, _ in PLAN]
 
     def place_of(k, held):
-        span = pl.ds(begins[k], begins[k + 1] - begins[k])
-        return tuple(held.get(d, slice(None)) for d in "ycvux") + (span,)
+        return tuple(held.get(d, slice(None)) for d in "ycvux") + (pl.ds(begins[k], sizes[k]),)
+
+    def land(k, i):
+        n = sum(steps[:k]) + i
+        return landing[n], step_sem.at[k], step_sem.at[len(PLAN) + n]
 
     def exchange(k, i):
-        order = PLAN[k][0]
-        held = {d: at_axis[d] for d in order[:i]}
-        held[order[i]] = 1 - at_axis[order[i]]
-        return send(
-            part.at[place_of(k, held)], landing[4 * k + i], class_sem, 4 * k + i, across[order[i]]
-        )
+        head = PLAN[k][0]
+        came, out_sem, in_sem = land(k, i)
+        held = {d: at_axis[d] for d in head[:i]}
+        held[head[i]] = 1 - at_axis[head[i]]
+        return send(part.at[place_of(k, held)], came, out_sem, in_sem, device(head[i]))
 
     def last(k):
-        order = PLAN[k][0]
-        d = order[3]
-        held = {e: at_axis[e] for e in order}
-        there, here = held | {d: 1 - at_axis[d]}, held
-        return [
-            send(
-                part.at[place_of(k, there | {"c": core})],
-                landing[4 * k + 3].at[0],
-                class_sem,
-                4 * k + 3,
-                across[d],
-            ),
-            send(
-                part.at[place_of(k, there | {"c": 1 - core})],
-                landing[4 * k + 3].at[1],
-                fin_sem,
-                2 * k,
-                beside[d],
-            ),
-            send(
-                part.at[place_of(k, here | {"c": 1 - core})],
-                landing[4 * k + 3].at[2],
-                fin_sem,
-                2 * k + 1,
-                mate,
-            ),
-        ]
+        final = PLAN[k][1]
+        came, out_sem, in_sem = land(k, steps[k] - 1)
+        ways = [(flip, turned) for turned in (False, True) for flip in flips(final)]
+        copies = []
+        for n, (flip, turned) in enumerate(ways + [("", True)]):
+            held = {d: 1 - v if d in flip else v for d, v in at_axis.items()}
+            held["c"] = 1 - core if turned else core
+            copies.append(
+                send(part.at[place_of(k, held)], came.at[n], out_sem, in_sem, device(flip, turned))
+            )
+        return copies
+
+    def begin(k, i):
+        if i < steps[k] - 1:
+            exchange(k, i).start()
+        else:
+            for copy in last(k):
+                copy.start()
 
     def take(k, i):
-        order, came = PLAN[k][0], landing[4 * k + i]
-        held = {d: at_axis[d] for d in order[: i + 1]}
-        if i == 3:
-            for copy in last(k):
-                copy.wait()
-            size = begins[k + 1] - begins[k]
-            other = pl.ds(pl.multiple_of((1 - core) * (high - half) + begins[k], 16), size)
-            own = pl.ds(pl.multiple_of(core * (high - half) + begins[k], 16), size)
-            mine = part[place_of(k, held | {"c": core})].astype(jnp.float32)
-            full[other, :] = came[1].astype(jnp.float32) + came[2].astype(jnp.float32)
-            full[own, :] = mine + came[0].astype(jnp.float32)
+        head = PLAN[k][0]
+        came, out_sem, in_sem = land(k, i)
+        if i == steps[k] - 1:
+            send(came, came, out_sem, in_sem, mate).wait()
+            ways = came.shape[0] // 2
+            other = pl.ds(pl.multiple_of((1 - core) * (high - half) + begins[k], 16), sizes[k])
+            own = pl.ds(pl.multiple_of(core * (high - half) + begins[k], 16), sizes[k])
+            mine = part[place_of(k, at_axis | {"c": core})].astype(jnp.float32)
+            theirs = came[2 * ways].astype(jnp.float32)
+            for n in range(ways):
+                mine += came[n].astype(jnp.float32)
+                theirs += came[ways + n].astype(jnp.float32)
+            full[other, :] = theirs
+            full[own, :] = mine
             return
         exchange(k, i).wait()
+        held = {d: at_axis[d] for d in head[: i + 1]}
         free = [d for d in "ycvux" if d not in held]
         for pick in itertools.product(range(2), repeat=len(free)):
             at = place_of(k, held | dict(zip(free, pick)))
             part[at] = (part[at].astype(jnp.float32) + came[pick].astype(jnp.float32)).astype(
                 jnp.bfloat16
             )
-        if i == 2:
-            for copy in last(k):
-                copy.start()
-        else:
-            exchange(k, i + 1).start()
+        begin(k, i + 1)
 
     for k in range(len(PLAN)):
         if k not in dict(LATE):
-            exchange(k, 0).start()
+            begin(k, 0)
 
     def give(s, j):
-        return send(pooled.at[j, s], got.at[t, s], pool_sem, s * (owners - 1) + j, (g, peer(j)))
+        return send(
+            pooled.at[j, s], got.at[t, s], pool_sem.at[0, j], pool_sem.at[1, j], (g, peer(j))
+        )
 
     share = rows // owners
     for s in range(slots):
-        for copy in got_ids[s]:
-            copy.wait()
+        if s < 2:
+            got_ids[s].wait()
+        elif s == 2:
+            later = pl.ds(2, slots - 2)
+            pltpu.make_async_copy(idx_s.at[later], idx_s.at[later], smem_sem.at[2]).wait()
         if s + 1 < slots:
             fetch(s + 1).wait()
         if s + 2 < slots:
@@ -486,24 +491,25 @@
             for n in range(owners):
                 now = s * owners + n
                 todo = [p for p in POLLS if p[0] == now]
-                begin = [k for k, p in LATE if p == now]
-                if todo or begin:
+                fresh = [k for k, p in LATE if p == now]
+                if todo or fresh:
 
                     @pl.when(j == n)
                     def _():
                         for _, k, i in todo:
                             take(k, i)
-                        for k in begin:
-                            exchange(k, 0).start()
+                        for k in fresh:
+                            begin(k, 0)
 
         got[t, s] = pooled[owners - 1, s]
 
     tail = [(k, i) for now, k, i in POLLS if now >= slots * owners]
     for n, (k, i) in enumerate(tail):
-        if all(i == 3 for _, i in tail[n:]) and tail[n - 1][1] < 3:
-            for s in range(slots):
-                for j in range(owners - 1):
-                    give(s, j).wait()
+        if n == SORT:
+            for j in range(owners - 1):
+                send(
+                    pooled.at[j], got.at[peer(j)], pool_sem.at[0, j], pool_sem.at[1, j], (g, peer(j))
+                ).wait()
             loads[7].wait()
             for f in range(feats):
                 s = slot_s[0, f]
@@ -528,11 +534,11 @@
     in_hbm = pl.BlockSpec(memory_space=pltpu.HBM)
     idx_shape = (owners, next_ids.shape[1] // owners, batch)
     vmem = pl.BlockSpec(memory_space=pltpu.VMEM)
-    landing = [
-        pltpu.VMEM(((2,) * (4 - i) if i < 3 else (3,)) + (n * half // 14, LANES), bf16)
-        for _, n in PLAN
-        for i in range(4)
-    ]
+    landing = []
+    for head, final, n in PLAN:
+        rows_of = (n * half // 14, LANES)
+        landing += [pltpu.VMEM((2,) * (4 - i) + rows_of, bf16) for i in range(len(head))]
+        landing.append(pltpu.VMEM((2 * len(flips(final)) + 1,) + rows_of, bf16))
     return pl.pallas_call(
         functools.partial(step_kernel, maxlen, factor),
         out_shape=(
@@ -550,8 +556,8 @@
             pltpu.VMEM(cotangent.shape, bf16),
             pltpu.VMEM(up_weight.shape, bf16),
             pltpu.VMEM(down_weight.shape, bf16),
-            pltpu.VMEM((depth, batch), bf16),
-            pltpu.VMEM((depth, batch), bf16),
+            pltpu.VMEM((groups, high, batch), bf16),
+            pltpu.VMEM((groups, high, batch), bf16),
             pltpu.VMEM((groups, half, batch), bf16),
             pltpu.VMEM((groups, half, batch), bf16),
             pltpu.VMEM((batch, rank), bf16),
@@ -571,12 +577,11 @@
             pltpu.VMEM((owners, slots, batch, width), bf16),
             pltpu.VMEM((owners, slots, batch, width), bf16),
             sems((2,)),
-            sems((slots * owners,)),
+            sems((3,)),
+            sems((2,)),
+            sems((2, 4)),
+            sems((len(PLAN) + len(landing),)),
             sems((2, owners - 1)),
-            sems((2, 2 * groups + 2)),
-            sems((2, 4 * len(PLAN))),
-            sems((2, 2 * len(PLAN))),
-            sems((2, slots * (owners - 1))),
             sems((8,)),
         ]
         + landing,

time: 37.3 us -> 35.6 us (0.954)
  Pallas kernels: 36.5 us -> 34.8 us
    pallas_call x1, Pallas kernels: 35.5 us -> 33.8 us  [fused_step(): pl.pallas_call(functools.partial(step_kernel, maxlen, factor), out_shape=...]
where the time goes in v5:
time: 35.6 us; the launch traced here: 35.5 us
  Pallas kernels  34.8 us (98%)
  between operations  0.64 us (2%)
    pallas_call x1, Pallas kernels, fused_step(): pl.pallas_call(functools.partial(step_kernel, maxlen, factor), out_shape=...  33.8 us
    pallas_call x1, Pallas kernels, finish(): pl.pallas_call(finish_kernel, out_shape=(jax.ShapeDtypeStruct(emb.shape,...  1.01 us

profile of v5, /device:TPU:0, one launch (start us, length us, event | category | flops | bytes accessed | tf_op | source)
XLA Modules:
  0.0 35.5 jit_solution(8651768312150366055)
XLA Ops:
  0.6 33.8 %fused_step.1 = (bf16[128,3328]{1,0:T(8,128)(2,1)S(1)}, f32[2,64,432]{2,1,0:T(8,128)S(1)}) custom-call(s32[224,128]{1,0:T(8,128)} %bitcast.4, s32[26,128]{1,0:T(8,128)} %bitcast.5, s32[1,26]{1,0:T(1,128)} %bitcast.6, bf16[7,6144,128]{2,1,0:T(8,128)(2,1)} %tab_ref.1, bf16[128,3456]{1,0:T(8,128)(2,1)} %x_hbm.1, bf16[128,3456]{1,0:T(8,128)(2,1)} %ct_hbm.1, ...), custom_call_target="tpu_custom_call" | custom-call | tf_op jit(solution)/shard_map/fused_step/pallas_call | solution.py:542
  34.5 1.0 %finish.1 = (bf16[128,3328]{1,0:T(8,128)(2,1)}, f32[64,432]{1,0:T(8,128)}, f32[64,432]{1,0:T(8,128)}) custom-call(bf16[128,3328]{1,0:T(8,128)(2,1)S(1)} %get-tuple-element.8.emb_in, f32[2,64,432]{2,1,0:T(8,128)S(1)} %get-tuple-element.9.sum_in), custom_call_target="tpu_custom_call" | custom-call | tf_op jit(solution)/shard_map/finish/pallas_call | solution.py:625

commit v6 on v5

--- a/solution.py
+++ b/solution.py
@@ -149,10 +149,10 @@
     return (next_embedded, grad_up, grad_down)
 
 
-PLAN = (("uxy", "v", 3), ("xy", "vu", 2), ("vux", "y", 3), ("xuv", "y", 4), ("yxu", "v", 2))
-POLLS = ((11, 3, 0), (13, 4, 0), (15, 0, 0), (16, 2, 0), (18, 1, 0), (19, 4, 1), (19, 3, 1), (22, 0, 1), (24, 1, 1), (25, 4, 2), (25, 2, 1), (28, 0, 2), (28, 3, 2), (28, 2, 2), (28, 4, 3), (28, 1, 2), (28, 3, 3), (28, 0, 3), (28, 2, 3))
-LATE = ((1, 8), (4, 1))
-SORT = 3
+PLAN = (("vyu", "x", 2), ("xu", "vy", 2), ("yxv", "u", 3), ("xuy", "v", 4), ("uv", "xy", 3))
+POLLS = ((11, 3, 0), (12, 0, 0), (13, 4, 0), (15, 2, 0), (19, 1, 0), (20, 0, 1), (22, 2, 1), (22, 3, 1), (27, 0, 2), (27, 4, 1), (27, 1, 1), (28, 3, 2), (28, 2, 2), (28, 0, 3), (28, 2, 3), (28, 4, 2), (28, 1, 2), (28, 3, 3))
+LATE = ((1, 10),)
+SORT = 2
 
 
 def flips(final):

time: 35.6 us -> 34.9 us (0.980)
  Pallas kernels: 34.8 us -> 34.1 us
    pallas_call x1, Pallas kernels: 33.8 us -> 33.1 us  [fused_step(): pl.pallas_call(functools.partial(step_kernel, maxlen, factor), out_shape=...]
where the time goes in v6:
time: 34.9 us; the launch traced here: 34.7 us
  Pallas kernels  34.1 us (98%)
  between operations  0.64 us (2%)
    pallas_call x1, Pallas kernels, fused_step(): pl.pallas_call(functools.partial(step_kernel, maxlen, factor), out_shape=...  33.1 us
    pallas_call x1, Pallas kernels, finish(): pl.pallas_call(finish_kernel, out_shape=(jax.ShapeDtypeStruct(emb.shape,...  1.01 us

profile of v6, /device:TPU:0, one launch (start us, length us, event | category | flops | bytes accessed | tf_op | source)
XLA Modules:
  0.0 34.7 jit_solution(17482121771557672968)
XLA Ops:
  0.6 33.1 %fused_step.1 = (bf16[128,3328]{1,0:T(8,128)(2,1)S(1)}, f32[2,64,432]{2,1,0:T(8,128)S(1)}) custom-call(s32[224,128]{1,0:T(8,128)} %bitcast.4, s32[26,128]{1,0:T(8,128)} %bitcast.5, s32[1,26]{1,0:T(1,128)} %bitcast.6, bf16[7,6144,128]{2,1,0:T(8,128)(2,1)} %tab_ref.1, bf16[128,3456]{1,0:T(8,128)(2,1)} %x_hbm.1, bf16[128,3456]{1,0:T(8,128)(2,1)} %ct_hbm.1, ...), custom_call_target="tpu_custom_call" | custom-call | tf_op jit(solution)/shard_map/fused_step/pallas_call | solution.py:542
  33.7 1.0 %finish.1 = (bf16[128,3328]{1,0:T(8,128)(2,1)}, f32[64,432]{1,0:T(8,128)}, f32[64,432]{1,0:T(8,128)}) custom-call(bf16[128,3328]{1,0:T(8,128)(2,1)S(1)} %get-tuple-element.8.emb_in, f32[2,64,432]{2,1,0:T(8,128)S(1)} %get-tuple-element.9.sum_in), custom_call_target="tpu_custom_call" | custom-call | tf_op jit(solution)/shard_map/finish/pallas_call | solution.py:625
